TPU v7x, 32 devices: a whole 2x2x4 slice. The times are simulated.
32 devices in a mesh: lam: 16 (over z, x, core), atom: 2 (over y).
Axes of the slice: x: 2, y: 2, z: 4, core: 2. Of those that a mesh axis runs over, the one named last changes fastest.
Arguments:
- coords: float32 [16, 3, 16384], P('lam', None, 'atom'), may hold values from 0 to 1
- velocities: float32 [16, 3, 16384], P('lam', None, 'atom'), may hold values from -6 to 6
- coupling: float32 [16, 2, 16384], P('lam', None, 'atom'), may hold values from 0.2 to 1
- charges: float32 [16384], replicated, may hold values from -1.5 to 1.5
- types: int32 [16384], replicated, may hold values from 0 to 15
- type_sigma: float32 [16], replicated, may hold values from 0.25 to 0.4
- type_eps: float32 [16], replicated, may hold values from 0.1 to 1
- near_tiles: int32 [128, 5], P('atom'), may hold values from 0 to 127
- accept: int32 [16], replicated, may hold values from 0 to 1, as said below
Outputs:
- energies: float32 [16, 3], P('lam')
- forces: float32 [16, 3, 16384], P('lam', None, 'atom')
- new_coords: float32 [16, 3, 16384], P('lam', None, 'atom')
- new_velocities: float32 [16, 3, 16384], P('lam', None, 'atom')
Inputs may be any that keep to these rules, and one draw needn't show every extreme that they name: accept[r] = 1 exchanges replicas r and r + 1 (modulo 16); no two consecutive entries around the cycle are both 1.
All inputs are finite; a program needn't handle non-finite values.
Results may differ from a plain program's by a relative error of at most 0.0003.
Values sent between devices are 32-bit elements; how exact they have to be, the bound alone decides.
A program may use at most 64 MiB of HBM per device.

v0:
```python
from functools import partial
import math

import jax
import jax.numpy as jnp
from jax import lax
from jax.sharding import PartitionSpec as P

TILE = 128


DELTA_SOFT = 0.05


def passed_along(x, axis, by):
    peers = lax.axis_size(axis)
    return lax.ppermute(x, axis, [(i, (i + by) % peers) for i in range(peers)])


def atom_params(charges, types, type_sigma, type_eps, coupling_whole):
    levels = lax.broadcasted_iota(jnp.int32, (type_sigma.shape[0], types.shape[0]), 0)
    onehot = (levels == types[None, :]).astype(jnp.float32)
    table = jnp.stack([type_sigma, jnp.sqrt(type_eps)])
    looked = jnp.dot(table, onehot, precision=lax.Precision.HIGHEST)
    return jnp.stack([charges * coupling_whole[0], looked[1] * coupling_whole[1], looked[0]])


def pair_block(inputs, with_force):
    rows_pos, cols_pos, rows_par, cols_par, rows_idx, cols_idx = inputs
    delta = rows_pos[:, :, None, :, None] - cols_pos[:, :, :, None, :]
    squared = jnp.sum(delta * delta, axis=0)
    charge_pair = rows_par[0][:, None, :, None] * cols_par[0][:, :, None, :]
    depth_pair = rows_par[1][:, None, :, None] * cols_par[1][:, :, None, :]
    sigma_pair = 0.5 * (rows_par[2][:, None, :, None] + cols_par[2][:, :, None, :])
    sigma_area = sigma_pair * sigma_pair
    pair_keep = (rows_idx[:, None, :, None] != cols_idx[:, :, None, :]).astype(jnp.float32)
    inverse = lax.rsqrt(squared + DELTA_SOFT)
    ratio = sigma_area / (squared + sigma_area)
    cubed = ratio * ratio * ratio
    energy_pair = charge_pair * inverse + 4.0 * depth_pair * (cubed * cubed - cubed)
    total = jnp.sum(energy_pair * pair_keep)
    if not with_force:
        return (total, jnp.zeros_like(rows_pos))
    slope = (
        -0.5 * charge_pair * inverse * inverse * inverse
        - 4.0
        * depth_pair
        * (6.0 * cubed * ratio * ratio - 3.0 * ratio * ratio)
        * ratio
        * ratio
        / sigma_area
    )
    weight = -2.0 * slope * pair_keep
    force = jnp.sum(weight[None] * delta, axis=(2, 4))
    return (total, force)


def evaluate(own_rows, whole, params, first_row, tile_list, with_force):
    count = own_rows.shape[1]
    row_tiles = count // TILE
    group = math.gcd(row_tiles, 4)
    blocks = row_tiles // group
    listed = tile_list.shape[1]
    rows_pos = own_rows.reshape(3, blocks, group, TILE).transpose(1, 0, 2, 3)
    own_par = lax.dynamic_slice_in_dim(params, first_row, count, 1)
    rows_par = own_par.reshape(3, blocks, group, TILE).transpose(1, 0, 2, 3)
    cols_pos = (
        whole.reshape(3, -1, TILE)[:, tile_list]
        .reshape(3, blocks, group, listed, TILE)
        .transpose(1, 0, 2, 3, 4)
    )
    cols_par = (
        params.reshape(3, -1, TILE)[:, tile_list]
        .reshape(3, blocks, group, listed, TILE)
        .transpose(1, 0, 2, 3, 4)
    )
    rows_idx = (first_row + jnp.arange(count, dtype=jnp.int32)).reshape(blocks, group, TILE)
    cols_idx = (
        tile_list[:, :, None] * TILE + jnp.arange(TILE, dtype=jnp.int32)[None, None, :]
    ).reshape(blocks, group, listed, TILE)
    totals, forces = lax.map(
        partial(pair_block, with_force=with_force),
        (rows_pos, cols_pos, rows_par, cols_par, rows_idx, cols_idx),
    )
    return (jnp.sum(totals), forces.transpose(1, 0, 2, 3).reshape(3, count))


def per_device(
    coords, velocities, coupling, charges, types, type_sigma, type_eps, near_tiles, accept
):
    own_coords = coords[0]
    moving = velocities[0]
    width = own_coords.shape[1]
    first_row = lax.axis_index("atom") * width
    whole_own, whole_coupling = (
        lax.all_gather(own_coords, "atom", axis=1, tiled=True),
        lax.all_gather(coupling[0], "atom", axis=1, tiled=True),
    )
    params = atom_params(charges, types, type_sigma, type_eps, whole_coupling)
    lower_coords, lower_moving = passed_along((own_coords, moving), "lam", 1)
    upper_coords, upper_moving = passed_along((own_coords, moving), "lam", -1)
    lower_whole, upper_whole = (
        lax.all_gather(lower_coords, "atom", axis=1, tiled=True),
        lax.all_gather(upper_coords, "atom", axis=1, tiled=True),
    )
    energy_own, force = evaluate(own_coords, whole_own, params, first_row, near_tiles, True)
    energy_low, unused = evaluate(lower_coords, lower_whole, params, first_row, near_tiles, False)
    energy_up, unused = evaluate(upper_coords, upper_whole, params, first_row, near_tiles, False)
    scale = 0.5 / (width * lax.axis_size("atom"))
    energy_own, energy_low, energy_up = lax.psum(
        (energy_own * scale, energy_low * scale, energy_up * scale), "atom"
    )
    from_upper = passed_along(energy_low, "lam", -1)
    from_lower = passed_along(energy_up, "lam", 1)
    energies = jnp.stack([energy_own, from_lower, from_upper])[None]
    replica = lax.axis_index("lam")
    cycle_size = lax.axis_size("lam")
    upper_flag = accept[replica] == 1
    lower_flag = accept[(replica + cycle_size - 1) % cycle_size] == 1
    new_coords = jnp.where(
        upper_flag, upper_coords, jnp.where(lower_flag, lower_coords, own_coords)
    )
    new_velocities = jnp.where(
        upper_flag, upper_moving, jnp.where(lower_flag, lower_moving, moving)
    )
    return (energies, force[None], new_coords[None], new_velocities[None])


def solution(mesh):
    in_specs = (
        P("lam", None, "atom"),
        P("lam", None, "atom"),
        P("lam", None, "atom"),
        P(),
        P(),
        P(),
        P(),
        P("atom", None),
        P(),
    )
    out_specs = (
        P("lam", None),
        P("lam", None, "atom"),
        P("lam", None, "atom"),
        P("lam", None, "atom"),
    )
    return jax.shard_map(
        per_device, mesh=mesh, in_specs=in_specs, out_specs=out_specs, check_vma=False
    )
```

profile of v0, /device:TPU:0, one launch (start us, length us, event | category | flops | bytes accessed | tf_op | source)
XLA Modules:
  0.0 263.5 jit_solution(11910193842850891822)
XLA Ops:
  2.3 5.4 %collective-permute-start = (f32[3,8192]{1,0:T(4,128)}, f32[3,8192]{1,0:T(4,128)S(1)}, u32[]{:S(2)}, u32[]{:S(2)}) collective-permute-start(f32[3,8192]{1,0:T(4,128)} %bitcast.145), channel_id=1, source_target_pairs={{0,30},{2,0},{4,2},{6,4},{8,6},{10,8},{12,10},{14,12},{16,14},{18,... | collective-permute-start | bytes 294920 | tf_op jit(solution)/shard_map/ppermute | solution.py:17
  9.3 4.4 %collective-permute-start.4 = (f32[3,8192]{1,0:T(4,128)}, f32[3,8192]{1,0:T(4,128)}, u32[]{:S(2)}, u32[]{:S(2)}) collective-permute-start(f32[3,8192]{1,0:T(4,128)} %bitcast.144), channel_id=1, source_target_pairs={{0,30},{2,0},{4,2},{6,4},{8,6},{10,8},{12,10},{14,12},{16,14},{18,... | collective-permute-start | bytes 294920 | tf_op jit(solution)/shard_map/ppermute | solution.py:17
  13.8 5.9 %all-gather.1 = f32[1,3,16384]{2,0,1:T(1,128)S(1)} all-gather(f32[1,3,8192]{2,0,1:T(1,128)} %param.15), channel_id=3, replica_groups=mesh['lam'=16,'atom'=2] {'atom'}, dimensions={2}, use_global_device_ids=true | all-gather | bytes 294912 | tf_op jit(solution)/shard_map/all_gather | solution.py:96
  19.7 5.1 %all-gather = f32[1,2,16384]{2,1,0:T(2,128)S(1)} all-gather(f32[1,2,8192]{2,1,0:T(2,128)} %param.17), channel_id=2, replica_groups=mesh['lam'=16,'atom'=2] {'atom'}, dimensions={2}, use_global_device_ids=true | all-gather | bytes 196608 | tf_op jit(solution)/shard_map/all_gather | solution.py:97
  27.9 2.0 gather_fusion
  30.6 2.0 gather_fusion.1
  32.7 73.3 %while.32 = (s32[]{:T(128)}, f32[16]{0:T(128)S(1)}, f32[16,3,4,128]{3,2,1,0:T(4,128)S(1)}, s32[16,4,128]{2,1,0:T(4,128)S(1)}, s32[16,4,5,128]{3,2,1,0:T(8,128)S(...) while((s32[]{:T(128)}, f32[16]{0:T(128)S(1)}, ...), condition=%wide.region_4.5_spmd, body=%wide.region_0.4_spmd.sunk | while | flops 17365508 | bytes 5617873 | solution.py:81
  33.4 2.5 compare_select_fusion.4
  37.9 2.5 compare_select_fusion.4
  42.5 2.5 compare_select_fusion.4
  47.1 2.5 compare_select_fusion.4
  51.7 2.5 compare_select_fusion.4
  56.3 2.5 compare_select_fusion.4
  60.8 2.5 compare_select_fusion.4
  65.4 2.5 compare_select_fusion.4
  70.0 2.5 compare_select_fusion.4
  74.6 2.5 compare_select_fusion.4
  79.1 2.5 compare_select_fusion.4
  83.7 2.5 compare_select_fusion.4
  88.3 2.5 compare_select_fusion.4
  92.9 2.5 compare_select_fusion.4
  97.5 2.5 compare_select_fusion.4
  102.0 2.5 compare_select_fusion.4
  109.8 5.6 %all_gather.14 = f32[3,16384]{1,0:T(4,128)S(1)} all-gather(f32[3,8192]{1,0:T(4,128)S(1)} %collective-permute-done), channel_id=1, replica_groups=mesh['lam'=16,'atom'=2] {'atom'}, dimensions={1}, use_global_device_ids=true | all-gather | bytes 294912 | tf_op jit(solution)/shard_map/all_gather | solution.py:104
  115.5 2.0 gather_fusion.2
  118.3 59.7 %while.33 = (s32[]{:T(128)}, f32[16]{0:T(128)S(1)}, s32[16,4,128]{2,1,0:T(4,128)S(1)}, s32[16,4,5,128]{3,2,1,0:T(8,128)S(1)}, f32[16,3,4,128]{3,2,1,0:T(4,128)S(...) while((s32[]{:T(128)}, f32[16]{0:T(128)S(1)}, ...), condition=%wide.region_10.11_spmd, body=%wide.region_7.10_spmd.sunk | while | flops 8847363 | bytes 2941125 | solution.py:81
  119.6 1.7 fusion.56
  123.3 1.7 fusion.56
  127.0 1.7 fusion.56
  130.8 1.7 fusion.56
  134.5 1.7 fusion.56
  138.2 1.7 fusion.56
  142.0 1.7 fusion.56
  145.7 1.7 fusion.56
  149.4 1.7 fusion.56
  153.2 1.7 fusion.56
  156.9 1.7 fusion.56
  160.6 1.7 fusion.56
  164.4 1.7 fusion.56
  168.1 1.7 fusion.56
  171.8 1.7 fusion.56
  175.5 1.7 fusion.56
  179.3 5.6 %all_gather.15 = f32[3,16384]{1,0:T(4,128)S(1)} all-gather(f32[3,8192]{1,0:T(4,128)S(1)} %collective-permute-done.2), channel_id=1, replica_groups=mesh['lam'=16,'atom'=2] {'atom'}, dimensions={1}, use_global_device_ids=true | all-gather | bytes 294912 | tf_op jit(solution)/shard_map/all_gather | solution.py:103
  184.9 2.0 gather_fusion.3
  187.7 59.8 %while.34 = (s32[]{:T(128)}, f32[16]{0:T(128)S(1)}, s32[16,4,128]{2,1,0:T(4,128)S(1)}, s32[16,4,5,128]{3,2,1,0:T(8,128)S(1)}, f32[16,3,4,128]{3,2,1,0:T(4,128)S(...) while((s32[]{:T(128)}, f32[16]{0:T(128)S(1)}, ...), condition=%wide.region_16.17_spmd, body=%wide.region_13.16_spmd.sunk | while | flops 8847363 | bytes 2941125 | solution.py:81
  189.0 1.7 fusion.59
  192.8 1.7 fusion.59
  196.5 1.7 fusion.59
  200.2 1.7 fusion.59
  204.0 1.7 fusion.59
  207.7 1.7 fusion.59
  211.5 1.7 fusion.59
  215.2 1.7 fusion.59
  218.9 1.7 fusion.59
  222.7 1.7 fusion.59
  226.4 1.7 fusion.59
  230.1 1.7 fusion.59
  233.9 1.7 fusion.59
  237.6 1.7 fusion.59
  241.4 1.7 fusion.59
  245.1 1.7 fusion.59
  248.8 6.1 %all-reduce = (f32[]{:T(128)}, f32[]{:T(128)}, f32[1]{0:T(128)}) all-reduce(f32[]{:T(128)S(6)} %mul.354, f32[]{:T(128)S(6)} %mul.353, f32[1]{0:T(128)} %bitcast.59), channel_id=1, replica_groups=mesh['lam'=16,'atom'=2] {'atom'}, use_global_device_ids=true, to_apply=%region_18.19 | all-reduce | flops 3 | bytes 24 | tf_op jit(solution)/shard_map/psum | solution.py:110
  254.9 4.4 %collective-permute-start.3 = (f32[]{:T(128)}, f32[]{:T(128)}, u32[]{:S(2)}, u32[]{:S(2)}) collective-permute-start(f32[]{:T(128)} %get-tuple-element.265), channel_id=1, source_target_pairs={{0,30},{2,0},{4,2},{6,4},{8,6},{10,8},{12,10},{14,12},{16,14},{18,... | collective-permute-start | bytes 20 | tf_op jit(solution)/shard_map/ppermute | solution.py:17
  261.0 2.5 maximum_bitcast_fusion
  (524 shorter events, 108.7 us)
Async XLA Ops:
  0.6 26.4 %copy-start.2 = (f32[16384]{0:T(1024)S(1)}, f32[16384]{0:T(1024)}, u32[]{:S(2)}) copy-start(f32[16384]{0:T(1024)} %param.18) | copy-start | bytes 196612
  2.3 25.2 %copy-start.3 = (s32[64,5]{0,1:T(8,128)S(1)}, s32[64,5]{0,1:T(8,128)}, u32[]{:S(2)}) copy-start(s32[64,5]{0,1:T(8,128)} %param.22) | copy-start | bytes 3844
  2.3 107.5 %collective-permute-start = (f32[3,8192]{1,0:T(4,128)}, f32[3,8192]{1,0:T(4,128)S(1)}, u32[]{:S(2)}, u32[]{:S(2)}) collective-permute-start(f32[3,8192]{1,0:T(4,128)} %bitcast.145), channel_id=1, source_target_pairs={{0,30},{2,0},{4,2},{6,4},{8,6},{10,8},{12,10},{14,12},{16,14},{18,... | collective-permute-start | bytes 294920 | tf_op jit(solution)/shard_map/ppermute | solution.py:17
  7.7 171.5 %collective-permute-start.2 = (f32[3,8192]{1,0:T(4,128)}, f32[3,8192]{1,0:T(4,128)S(1)}, u32[]{:S(2)}, u32[]{:S(2)}) collective-permute-start(f32[3,8192]{1,0:T(4,128)} %bitcast.145), channel_id=1, source_target_pairs={{0,2},{2,4},{4,6},{6,8},{8,10},{10,12},{12,14},{14,16},{16,18},{18... | collective-permute-start | bytes 294920 | tf_op jit(solution)/shard_map/ppermute | solution.py:17
  9.3 250.8 %collective-permute-start.4 = (f32[3,8192]{1,0:T(4,128)}, f32[3,8192]{1,0:T(4,128)}, u32[]{:S(2)}, u32[]{:S(2)}) collective-permute-start(f32[3,8192]{1,0:T(4,128)} %bitcast.144), channel_id=1, source_target_pairs={{0,30},{2,0},{4,2},{6,4},{8,6},{10,8},{12,10},{14,12},{16,14},{18,... | collective-permute-start | bytes 294920 | tf_op jit(solution)/shard_map/ppermute | solution.py:17
  13.8 246.4 %collective-permute-start.5 = (f32[3,8192]{1,0:T(4,128)}, f32[3,8192]{1,0:T(4,128)}, u32[]{:S(2)}, u32[]{:S(2)}) collective-permute-start(f32[3,8192]{1,0:T(4,128)} %bitcast.144), channel_id=1, source_target_pairs={{0,2},{2,4},{4,6},{6,8},{8,10},{10,12},{12,14},{14,16},{16,18},{18... | collective-permute-start | bytes 294920 | tf_op jit(solution)/shard_map/ppermute | solution.py:17
  30.6 2.1 copy-start
  32.7 73.3 %copy-start.4 = (s32[16]{0:T(128)S(1)}, s32[16]{0:T(128)}, u32[]{:S(2)}) copy-start(s32[16]{0:T(128)} %param.23) | copy-start | bytes 196
  187.7 72.5 %copy-start.1 = (f32[1,3,8192]{2,0,1:T(1,128)S(1)}, f32[1,3,8192]{2,0,1:T(1,128)}, u32[]{:S(2)}) copy-start(f32[1,3,8192]{2,0,1:T(1,128)} %param.16) | copy-start | bytes 294916
  254.9 6.1 %collective-permute-start.1 = (f32[]{:T(128)}, f32[]{:T(128)}, u32[]{:S(2)}, u32[]{:S(2)}) collective-permute-start(f32[]{:T(128)} %get-tuple-element.266), channel_id=1, source_target_pairs={{0,2},{2,4},{4,6},{6,8},{8,10},{10,12},{12,14},{14,16},{16,18},{18... | collective-permute-start | bytes 20 | tf_op jit(solution)/shard_map/ppermute | solution.py:17
  254.9 6.1 %collective-permute-start.3 = (f32[]{:T(128)}, f32[]{:T(128)}, u32[]{:S(2)}, u32[]{:S(2)}) collective-permute-start(f32[]{:T(128)} %get-tuple-element.265), channel_id=1, source_target_pairs={{0,30},{2,0},{4,2},{6,4},{8,6},{10,8},{12,10},{14,12},{16,14},{18,... | collective-permute-start | bytes 20 | tf_op jit(solution)/shard_map/ppermute | solution.py:17
where the time goes:
time: 266 us; the launch traced here: 263 us
  other arithmetic  133 us (50%)
  local copies, waits for them, and re-layouts  79 us (30%)
  blocking collectives  28.5 us (11%)
  starting transfers between devices  14.3 us (5%)
  between operations  4.17 us (2%)
  loops' own time  2.78 us (1%)
    reduce_sum x32, other arithmetic, pair_block(): total = jnp.sum(energy_pair * pair_keep)  54.9 us
    mul x16, other arithmetic, pair_block(): weight = -2.0 * slope * pair_keep  39.7 us
    dynamic_update_slice x64, local copies, waits for them, and re-layouts, evaluate(): lax.map(partial(pair_block, with_force=with_force), (rows_pos, cols_pos,...  35.9 us
    sub x48, local copies, waits for them, and re-layouts, pair_block(): delta = rows_pos[:, :, None, :, None] - cols_pos[:, :, :, None, :]  22.6 us
    reduce_sum x48, other arithmetic, pair_block(): squared = jnp.sum(delta * delta, axis=0)  22.2 us
    ppermute x6, starting transfers between devices, passed_along(): return lax.ppermute(x, axis, [(i, (i + by) % peers) for i in range(peers)])  14.3 us
    reduce_sum x16, other arithmetic, pair_block(): force = jnp.sum(weight[None] * delta, axis=(2, 4))  11.4 us
    psum x1, blocking collectives, per_device(): lax.psum((energy_own * scale, energy_low * scale, energy_up * scale), 'at...  6.1 us
  transfers between devices with their start and end apart: 6, of which 0 were waited for; matrix products, arithmetic and copies ran while one was open for 80% of the time, Pallas kernels for 0%

commit v1 on v0

v1 whole, which is shorter than its diff:
```python
from functools import partial

import jax
import jax.numpy as jnp
from jax import lax
from jax.experimental import pallas as pl
from jax.experimental.pallas import tpu as pltpu
from jax.sharding import PartitionSpec as P

TILE = 128
DELTA_SOFT = 0.05
SUB = 8


def moved(x, lam_by, atom_by):
    cycle, parts = lax.axis_size("lam"), lax.axis_size("atom")
    pairs = []
    for r in range(cycle):
        for a in range(parts):
            source = ((r - lam_by) % cycle) * parts + (a + atom_by) % parts
            pairs.append((source, r * parts + a))
    return lax.ppermute(x, ("lam", "atom"), pairs)


def tiles_kernel(parts, listed, *refs):
    where_ref, near_ref, sigma_ref, eps_ref, charges_ref, types_ref = refs[:6]
    halves = refs[6 : 6 + 4 * parts]
    force_ref, energy_ref, cols, turned, packed = refs[6 + 4 * parts :]
    width = halves[0].shape[2]
    row_tiles = width // TILE
    part = where_ref[0]

    kinds = types_ref[...]
    radius = jnp.zeros(kinds.shape, jnp.float32)
    depth = jnp.zeros(kinds.shape, jnp.float32)
    for level in range(sigma_ref.shape[0]):
        here = kinds == level
        radius = jnp.where(here, sigma_ref[level], radius)
        depth = jnp.where(here, eps_ref[level], depth)
    cols[3:4, :] = 0.5 * radius
    depth = 2.0 * jnp.sqrt(depth)
    cols[5:6, :] = depth
    cols[10:16, :] = jnp.zeros((6, kinds.shape[1]), jnp.float32)
    for step in range(parts):
        start = pl.multiple_of(lax.rem(part + step, parts) * width, TILE)
        span = pl.ds(start, width)
        cols[0:3, span] = halves[step][0]
    base = cols[5:6, :]
    for h in range(3):
        for step in range(parts):
            start = pl.multiple_of(lax.rem(part + step, parts) * width, TILE)
            span = pl.ds(start, width)
            scales = halves[parts * (h + 1) + step]
            cols[4 + 2 * h : 6 + 2 * h, span] = scales[0]
        cols[4 + 2 * h : 5 + 2 * h, :] = cols[4 + 2 * h : 5 + 2 * h, :] * charges_ref[...]
        cols[5 + 2 * h : 6 + 2 * h, :] = cols[5 + 2 * h : 6 + 2 * h, :] * base

    lane = lax.broadcasted_iota(jnp.int32, (SUB, TILE), 1)
    first_tile = part * row_tiles

    def row_tile(t, carry):
        totals, selfs = carry
        own = first_tile + t
        own_span = pl.ds(pl.multiple_of(own * TILE, TILE), TILE)
        turned[...] = cols[:, own_span].T
        near = [near_ref[t, k] for k in range(listed)]
        spans = [pl.ds(pl.multiple_of(n * TILE, TILE), TILE) for n in near]
        twice = jnp.float32(0.0)
        for n in near:
            twice = twice + (n == own).astype(jnp.float32)
        own_charge = [cols[4 + 2 * h : 5 + 2 * h, own_span] for h in range(3)]
        selfs = tuple(s + twice * (q * q) for s, q in zip(selfs, own_charge))

        def row_block(b, totals):
            rows = turned[pl.ds(pl.multiple_of(b * SUB, SUB), SUB), :]
            xi, yi, zi, ri, qi, ei, qa, ea, qb, eb = [
                jnp.broadcast_to(rows[:, c : c + 1], (SUB, TILE)) for c in range(10)
            ]
            e6 = 6.0 * ei
            sums = [None] * 9

            def put(slot, value):
                sums[slot] = value if sums[slot] is None else sums[slot] + value

            for span in spans:
                def col(c):
                    return jnp.broadcast_to(cols[c : c + 1, span], (SUB, TILE))

                dx, dy, dz = xi - col(0), yi - col(1), zi - col(2)
                s = dx * dx + dy * dy + dz * dz
                inv = lax.rsqrt(s + DELTA_SOFT)
                g = ri + col(3)
                area = g * g
                root = lax.rsqrt(s + area)
                p = root * root
                x = area * p
                x3 = x * x * x
                low = x3 - 1.0
                lj = x3 * low
                charge = col(4) * inv
                put(0, charge)
                put(1, col(5) * lj)
                put(2, col(6) * inv)
                put(3, col(7) * lj)
                put(4, col(8) * inv)
                put(5, col(9) * lj)
                w = qi * (charge * (inv * inv)) + (e6 * col(5)) * ((x3 * p) * (x3 + low))
                put(6, w * dx)
                put(7, w * dy)
                put(8, w * dz)
            fx, fy, fz = [jnp.sum(v, axis=1, keepdims=True) for v in sums[6:9]]
            packed[pl.ds(pl.multiple_of(b * SUB, SUB), SUB), :] = jnp.where(
                lane == 0, fx, jnp.where(lane == 1, fy, fz)
            )
            return (
                totals[0] + (qi * sums[0] + ei * sums[1]),
                totals[1] + (qa * sums[2] + ea * sums[3]),
                totals[2] + (qb * sums[4] + eb * sums[5]),
            )

        totals = lax.fori_loop(0, TILE // SUB, row_block, totals)
        out_span = pl.ds(pl.multiple_of(t * TILE, TILE), TILE)
        force_ref[0, :, out_span] = packed[...].T[0:3]
        return totals, selfs

    zero = jnp.zeros((SUB, TILE), jnp.float32)
    none = jnp.zeros((1, TILE), jnp.float32)
    totals, selfs = lax.fori_loop(0, row_tiles, row_tile, ((zero,) * 3, (none,) * 3))
    soft = lax.rsqrt(jnp.full((1, TILE), DELTA_SOFT, jnp.float32))
    lane1 = lax.broadcasted_iota(jnp.int32, (1, TILE), 1)
    line = jnp.zeros((1, TILE), jnp.float32)
    for h in range(3):
        value = jnp.sum(jnp.sum(totals[h], axis=0, keepdims=True) - selfs[h] * soft)
        line = jnp.where(lane1 == h, value, line)
    energy_ref[...] = line


def per_device(
    coords, velocities, coupling, charges, types, type_sigma, type_eps, near_tiles, accept
):
    parts, width = lax.axis_size("atom"), coords.shape[2]
    atoms = parts * width
    part = lax.axis_index("atom")
    halves = [coords] + [moved(coords, 0, step) for step in range(1, parts)]
    for by in (0, 1, -1):
        for step in range(parts):
            halves.append(coupling if by == step == 0 else moved(coupling, by, step))
    lower_coords, lower_moving = moved(coords, 1, 0), moved(velocities, 1, 0)
    upper_coords, upper_moving = moved(coords, -1, 0), moved(velocities, -1, 0)

    smem = pl.BlockSpec(memory_space=pltpu.SMEM)
    vmem = pl.BlockSpec(memory_space=pltpu.VMEM)
    pairs = width * near_tiles.shape[1] * TILE
    force, line = pl.pallas_call(
        partial(tiles_kernel, parts, near_tiles.shape[1]),
        out_shape=(
            jax.ShapeDtypeStruct(coords.shape, jnp.float32),
            jax.ShapeDtypeStruct((1, TILE), jnp.float32),
        ),
        in_specs=[smem] * 4 + [vmem] * (2 + len(halves)),
        out_specs=(vmem, vmem),
        scratch_shapes=[
            pltpu.VMEM((16, atoms), jnp.float32),
            pltpu.VMEM((TILE, 16), jnp.float32),
            pltpu.VMEM((TILE, TILE), jnp.float32),
        ],
        cost_estimate=pl.CostEstimate(
            flops=50 * pairs, bytes_accessed=4 * 20 * atoms, transcendentals=2 * pairs
        ),
        name="tiles",
    )(
        part.reshape(1).astype(jnp.int32),
        near_tiles,
        type_sigma,
        type_eps,
        charges.reshape(1, atoms),
        types.reshape(1, atoms),
        *halves,
    )
    shares = jnp.stack([line[0, :3]] + [moved(line, 0, step)[0, :3] for step in range(1, parts)])
    total = shares[0]
    for step in range(1, parts):
        total = total + shares[step]
    if parts > 2:
        order = (jnp.arange(parts) - part) % parts
        total = jnp.sum(shares[order], axis=0)
    energies = (total * (0.5 / atoms))[None]

    replica, cycle = lax.axis_index("lam"), lax.axis_size("lam")
    up = accept[replica] == 1
    low = accept[(replica + cycle - 1) % cycle] == 1
    new_coords = jnp.where(up, upper_coords, jnp.where(low, lower_coords, coords))
    new_velocities = jnp.where(up, upper_moving, jnp.where(low, lower_moving, velocities))
    return (energies, force, new_coords, new_velocities)


def solution(mesh):
    split = P("lam", None, "atom")
    return jax.shard_map(
        per_device,
        mesh=mesh,
        in_specs=(split, split, split, P(), P(), P(), P(), P("atom", None), P()),
        out_specs=(P("lam", None), split, split, split),
        check_vma=False,
    )
```

time: 266 us -> 260 us (0.977)
  Pallas kernels: 0 us -> 233 us
  other arithmetic: 133 us -> 2.07 us
  local copies, waits for them, and re-layouts: 79 us -> 5.77 us
  blocking collectives: 28.5 us -> 0 us
  loops' own time: 2.78 us -> 0 us
    pallas_call x0 -> x1, Pallas kernels: none -> 233 us  [per_device(): pl.pallas_call(partial(tiles_kernel, parts, near_tiles.shape[1]), out_sha...]
    reduce_sum x99 -> x0, other arithmetic: 90.3 us -> none  [the longest x32 54.9 us: pair_block(): total = jnp.sum(energy_pair * pair_keep)]
    mul x17 -> x1, other arithmetic: 39.7 us -> 0.51 us  [per_device(): energies = (total * (0.5 / atoms))[None]]
    dynamic_update_slice x64 -> x0, local copies, waits for them, and re-layouts: 35.9 us -> none  [evaluate(): lax.map(partial(pair_block, with_force=with_force), (rows_pos, cols_pos,...]
    sub x48 -> x0, local copies, waits for them, and re-layouts: 22.6 us -> none  [pair_block(): delta = rows_pos[:, :, None, :, None] - cols_pos[:, :, :, None, :]]
    all_gather x4 -> x0, blocking collectives: 22.4 us -> none  [the longest x1 5.94 us: per_device(): lax.all_gather(own_coords, 'atom', axis=1, tiled=True)]
    gather x8 -> x0, local copies, waits for them, and re-layouts: 8.14 us -> none  [the longest x6 6.1 us: evaluate(): whole.reshape(3, -1, TILE)[:, tile_list]]
    psum x1 -> x0, blocking collectives: 6.1 us -> none  [per_device(): lax.psum((energy_own * scale, energy_low * scale, energy_up * scale), 'at...]
  transfers between devices with their start and end apart: 6 -> 11, of which waited for: 0 -> 1; matrix products, arithmetic and copies ran while one was open for 80% -> 2% of each run, Pallas kernels for 0% -> 90%
where the time goes in v1:
time: 260 us; the launch traced here: 259 us
  Pallas kernels  233 us (90%)
  starting transfers between devices  16.3 us (6%)
  local copies, waits for them, and re-layouts  5.77 us (2%)
    pallas_call x1, Pallas kernels, per_device(): pl.pallas_call(partial(tiles_kernel, parts, near_tiles.shape[1]), out_sha...  233 us
    ppermute x11, starting transfers between devices, moved(): return lax.ppermute(x, ('lam', 'atom'), pairs)  16.3 us
  transfers between devices with their start and end apart: 11, of which 1 were waited for; matrix products, arithmetic and copies ran while one was open for 2% of the time, Pallas kernels for 90%

profile of v1, /device:TPU:0, one launch (start us, length us, event | category | flops | bytes accessed | tf_op | source)
XLA Modules:
  0.0 259.4 jit_solution(5582682151136232302)
XLA Ops:
  0.6 0.0 copy-start.7
  0.6 0.0 copy-start
  0.7 0.0 copy-start.3
  0.7 3.1 %collective-permute-start.1 = (f32[1,2,8192]{2,1,0:T(2,128)}, f32[1,2,8192]{2,1,0:T(2,128)S(1)}, u32[]{:S(2)}, u32[]{:S(2)}) collective-permute-start(f32[1,2,8192]{2,1,0:T(2,128)} %refs_8_.1), channel_id=1, source_target_pairs={{1,0},{0,1},{3,2},{2,3},{5,4},{4,5},{7,6},{6,7},{9,8},{8,9},{11,10... | collective-permute-start | bytes 196616 | tf_op jit(solution)/shard_map/ppermute | solution.py:22
  3.7 0.0 collective-permute-start.2
  3.7 1.7 collective-permute-start.3
  5.4 1.0 copy.15.refs_6_
  6.4 0.0 copy-start.1
  6.4 1.6 collective-permute-start
  8.0 0.0 copy-done
  8.0 2.4 collective-permute-start.7
  10.4 0.0 collective-permute-done.1.refs_9_
  10.4 0.0 copy-start.8
  10.4 0.0 collective-permute-start.8
  10.4 0.0 collective-permute-done.2.refs_10_
  10.4 0.0 copy-done.7
  10.4 0.0 copy-start.9
  10.4 4.5 %collective-permute-start.4 = (f32[1,2,8192]{2,1,0:T(2,128)S(1)}, f32[1,2,8192]{2,1,0:T(2,128)S(1)}, u32[]{:S(2)}, u32[]{:S(2)}) collective-permute-start(f32[1,2,8192]{2,1,0:T(2,128)S(1)} %copy-done.7), channel_id=1, source_target_pairs={{2,0},{3,1},{4,2},{5,3},{6,4},{7,5},{8,6},{9,7},{10,8},{11,9},{12,... | collective-permute-start | bytes 196616 | tf_op jit(solution)/shard_map/ppermute | solution.py:22
  14.9 0.0 collective-permute-done.3.refs_11_
  14.9 0.0 copy-start.10
  14.9 0.1 collective-permute-start.5
  15.0 0.0 copy-start.4
  15.0 0.7 copy-done.4
  15.7 0.7 copy.14.refs_1_
  16.4 0.0 copy-start.5
  16.4 0.7 copy-done.5
  17.0 0.6 fusion
  18.8 0.0 collective-permute-done.4.refs_12_
  18.8 0.0 copy-done.3
  18.8 0.0 copy-start.11
  18.9 2.4 collective-permute-start.9
  21.3 0.0 collective-permute-done.5.refs_13_
  21.3 0.0 copy-start.12
  21.3 0.0 collective-permute-start.10
  21.3 0.0 collective-permute-done.refs_7_
  21.3 0.0 copy-start.6
  21.3 0.0 copy-done.1
  21.3 0.0 copy-done.8
  21.3 0.0 copy-done.9
  21.4 0.0 copy-done.10
  21.4 0.0 copy-done.11
  21.4 0.5 copy-done.12
  21.9 0.0 copy-done.6
  22.0 232.7 %tiles.1 = (f32[1,3,8192]{2,1,0:T(4,128)}, f32[1,128]{1,0:T(1,128)}) custom-call(s32[1]{0:T(128)} %bitcast.refs_0_, s32[64,5]{1,0:T(8,128)} %copy.14.refs_1_, f32[16]{0:T(128)} %refs_2_.1, f32[16]{0:T(128)} %refs_3_.1, f32[1,16384]{1,0:T(1,128)} %bitcast.5, s32[1,16384]{1,0:T(1,128)} %bitcast.6, f32[1,3,8192]{2,1,0:T(4,128)} %copy-done.1, ...), custom_call_target="tpu_custom_call" | custom-call | flops 262144000 | bytes 1310720 | tf_op jit(solution)/shard_map/tiles/pallas_call | solution.py:154
  254.7 0.0 copy-start.13
  254.7 0.7 copy-done.13
  255.3 0.6 collective-permute-start.6
  255.9 0.0 collective-permute-done.7
  255.9 0.0 collective-permute-done.8
  255.9 0.8 broadcast_select_fusion.3
  256.7 0.0 copy-start.2
  256.7 0.0 collective-permute-done.9
  256.7 0.0 collective-permute-done.10
  256.7 0.8 broadcast_select_fusion.2
  257.5 0.1 copy-done.2
  257.6 0.7 copy.16
  258.3 0.6 collective-permute-done.6
  258.9 0.5 add_multiply_fusion
Async XLA Ops:
  0.6 9.8 %copy-start.7 = (f32[1,2,8192]{2,1,0:T(2,128)S(1)}, f32[1,2,8192]{2,1,0:T(2,128)}, u32[]{:S(2)}) copy-start(f32[1,2,8192]{2,1,0:T(2,128)} %refs_8_.1) | copy-start | bytes 196612
  0.6 7.4 %copy-start = (f32[1,3,8192]{2,0,1:T(1,128)S(1)}, f32[1,3,8192]{2,0,1:T(1,128)}, u32[]{:S(2)}) copy-start(f32[1,3,8192]{2,0,1:T(1,128)} %param.9) | copy-start | bytes 294916
  0.7 18.2 %copy-start.3 = (f32[1,3,8192]{2,0,1:T(1,128)S(1)}, f32[1,3,8192]{2,0,1:T(1,128)}, u32[]{:S(2)}) copy-start(f32[1,3,8192]{2,0,1:T(1,128)} %param.10) | copy-start | bytes 294916
  0.7 9.7 %collective-permute-start.1 = (f32[1,2,8192]{2,1,0:T(2,128)}, f32[1,2,8192]{2,1,0:T(2,128)S(1)}, u32[]{:S(2)}, u32[]{:S(2)}) collective-permute-start(f32[1,2,8192]{2,1,0:T(2,128)} %refs_8_.1), channel_id=1, source_target_pairs={{1,0},{0,1},{3,2},{2,3},{5,4},{4,5},{7,6},{6,7},{9,8},{8,9},{11,10... | collective-permute-start | bytes 196616 | tf_op jit(solution)/shard_map/ppermute | solution.py:22
  3.7 6.7 %collective-permute-start.2 = (f32[1,2,8192]{2,1,0:T(2,128)}, f32[1,2,8192]{2,1,0:T(2,128)S(1)}, u32[]{:S(2)}, u32[]{:S(2)}) collective-permute-start(f32[1,2,8192]{2,1,0:T(2,128)} %refs_8_.1), channel_id=1, source_target_pairs={{30,0},{31,1},{0,2},{1,3},{2,4},{3,5},{4,6},{5,7},{6,8},{7,9},{8,1... | collective-permute-start | bytes 196616 | tf_op jit(solution)/shard_map/ppermute | solution.py:22
  3.7 11.2 %collective-permute-start.3 = (f32[1,2,8192]{2,1,0:T(2,128)}, f32[1,2,8192]{2,1,0:T(2,128)S(1)}, u32[]{:S(2)}, u32[]{:S(2)}) collective-permute-start(f32[1,2,8192]{2,1,0:T(2,128)} %refs_8_.1), channel_id=1, source_target_pairs={{31,0},{30,1},{1,2},{0,3},{3,4},{2,5},{5,6},{4,7},{7,8},{6,9},{9,1... | collective-permute-start | bytes 196616 | tf_op jit(solution)/shard_map/ppermute | solution.py:22
  6.4 14.9 %copy-start.1 = (f32[1,3,8192]{2,1,0:T(4,128)}, f32[1,3,8192]{2,1,0:T(4,128)S(1)}, u32[]{:S(2)}) copy-start(f32[1,3,8192]{2,1,0:T(4,128)S(1)} %copy.15.refs_6_) | copy-start | bytes 294916
  6.4 14.9 %collective-permute-start = (f32[1,3,8192]{2,1,0:T(4,128)S(1)}, f32[1,3,8192]{2,1,0:T(4,128)S(1)}, u32[]{:S(2)}, u32[]{:S(2)}) collective-permute-start(f32[1,3,8192]{2,1,0:T(4,128)S(1)} %copy.15.refs_6_), channel_id=1, source_target_pairs={{1,0},{0,1},{3,2},{2,3},{5,4},{4,5},{7,6},{6,7},{9,8},{8,9},{11,10... | collective-permute-start | bytes 294920 | tf_op jit(solution)/shard_map/ppermute | solution.py:22
  8.0 247.9 %collective-permute-start.7 = (f32[1,3,8192]{2,0,1:T(1,128)S(1)}, f32[1,3,8192]{2,0,1:T(1,128)S(1)}, u32[]{:S(2)}, u32[]{:S(2)}) collective-permute-start(f32[1,3,8192]{2,0,1:T(1,128)S(1)} %copy-done), channel_id=1, source_target_pairs={{2,0},{3,1},{4,2},{5,3},{6,4},{7,5},{8,6},{9,7},{10,8},{11,9},{12,... | collective-permute-start | bytes 294920 | tf_op jit(solution)/shard_map/ppermute | solution.py:22
  10.4 10.9 %copy-start.8 = (f32[1,2,8192]{2,1,0:T(2,128)}, f32[1,2,8192]{2,1,0:T(2,128)S(1)}, u32[]{:S(2)}) copy-start(f32[1,2,8192]{2,1,0:T(2,128)S(1)} %collective-permute-done.1.refs_9_) | copy-start | bytes 196612
  10.4 245.5 %collective-permute-start.8 = (f32[1,3,8192]{2,0,1:T(1,128)S(1)}, f32[1,3,8192]{2,0,1:T(1,128)S(1)}, u32[]{:S(2)}, u32[]{:S(2)}) collective-permute-start(f32[1,3,8192]{2,0,1:T(1,128)S(1)} %copy-done), channel_id=1, source_target_pairs={{30,0},{31,1},{0,2},{1,3},{2,4},{3,5},{4,6},{5,7},{6,8},{7,9},{8,1... | collective-permute-start | bytes 294920 | tf_op jit(solution)/shard_map/ppermute | solution.py:22
  10.4 10.9 %copy-start.9 = (f32[1,2,8192]{2,1,0:T(2,128)}, f32[1,2,8192]{2,1,0:T(2,128)S(1)}, u32[]{:S(2)}) copy-start(f32[1,2,8192]{2,1,0:T(2,128)S(1)} %collective-permute-done.2.refs_10_) | copy-start | bytes 196612
  10.4 8.4 %collective-permute-start.4 = (f32[1,2,8192]{2,1,0:T(2,128)S(1)}, f32[1,2,8192]{2,1,0:T(2,128)S(1)}, u32[]{:S(2)}, u32[]{:S(2)}) collective-permute-start(f32[1,2,8192]{2,1,0:T(2,128)S(1)} %copy-done.7), channel_id=1, source_target_pairs={{2,0},{3,1},{4,2},{5,3},{6,4},{7,5},{8,6},{9,7},{10,8},{11,9},{12,... | collective-permute-start | bytes 196616 | tf_op jit(solution)/shard_map/ppermute | solution.py:22
  14.9 6.5 %copy-start.10 = (f32[1,2,8192]{2,1,0:T(2,128)}, f32[1,2,8192]{2,1,0:T(2,128)S(1)}, u32[]{:S(2)}) copy-start(f32[1,2,8192]{2,1,0:T(2,128)S(1)} %collective-permute-done.3.refs_11_) | copy-start | bytes 196612
  14.9 6.4 %collective-permute-start.5 = (f32[1,2,8192]{2,1,0:T(2,128)S(1)}, f32[1,2,8192]{2,1,0:T(2,128)S(1)}, u32[]{:S(2)}, u32[]{:S(2)}) collective-permute-start(f32[1,2,8192]{2,1,0:T(2,128)S(1)} %copy-done.7), channel_id=1, source_target_pairs={{3,0},{2,1},{5,2},{4,3},{7,4},{6,5},{9,6},{8,7},{11,8},{10,9},{13,... | collective-permute-start | bytes 196616 | tf_op jit(solution)/shard_map/ppermute | solution.py:22
  15.0 0.7 copy-start.4
  16.4 0.7 copy-start.5
  18.8 2.5 copy-start.11
  18.9 237.8 %collective-permute-start.9 = (f32[1,3,8192]{2,0,1:T(1,128)S(1)}, f32[1,3,8192]{2,0,1:T(1,128)S(1)}, u32[]{:S(2)}, u32[]{:S(2)}) collective-permute-start(f32[1,3,8192]{2,0,1:T(1,128)S(1)} %copy-done.3), channel_id=1, source_target_pairs={{2,0},{3,1},{4,2},{5,3},{6,4},{7,5},{8,6},{9,7},{10,8},{11,9},{12,... | collective-permute-start | bytes 294920 | tf_op jit(solution)/shard_map/ppermute | solution.py:22
  21.3 0.6 copy-start.12
  21.3 235.4 %collective-permute-start.10 = (f32[1,3,8192]{2,0,1:T(1,128)S(1)}, f32[1,3,8192]{2,0,1:T(1,128)S(1)}, u32[]{:S(2)}, u32[]{:S(2)}) collective-permute-start(f32[1,3,8192]{2,0,1:T(1,128)S(1)} %copy-done.3), channel_id=1, source_target_pairs={{30,0},{31,1},{0,2},{1,3},{2,4},{3,5},{4,6},{5,7},{6,8},{7,9},{8,1... | collective-permute-start | bytes 294920 | tf_op jit(solution)/shard_map/ppermute | solution.py:22
  21.3 0.6 copy-start.6
  254.7 0.7 copy-start.13
  255.3 3.6 %collective-permute-start.6 = (f32[1,128]{1,0:T(1,128)S(1)}, f32[1,128]{1,0:T(1,128)S(1)}, u32[]{:S(2)}, u32[]{:S(2)}) collective-permute-start(f32[1,128]{1,0:T(1,128)S(1)} %copy-done.13), channel_id=1, source_target_pairs={{1,0},{0,1},{3,2},{2,3},{5,4},{4,5},{7,6},{6,7},{9,8},{8,9},{11,10... | collective-permute-start | bytes 1544 | tf_op jit(solution)/shard_map/ppermute | solution.py:22
  256.7 0.9 copy-start.2

commit v2 on v1

v2 whole, which is shorter than its diff:
```python
from functools import partial

import jax
import jax.numpy as jnp
from jax import lax
from jax.experimental import pallas as pl
from jax.experimental.pallas import tpu as pltpu
from jax.sharding import PartitionSpec as P

TILE = 128
DELTA_SOFT = 0.05
SUB = 8
DEPTH = 48


def moved(x, lam_by, atom_by):
    cycle, parts = lax.axis_size("lam"), lax.axis_size("atom")
    pairs = []
    for r in range(cycle):
        for a in range(parts):
            source = ((r - lam_by) % cycle) * parts + (a + atom_by) % parts
            pairs.append((source, r * parts + a))
    return lax.ppermute(x, ("lam", "atom"), pairs)


def split3(x):
    high = x.astype(jnp.bfloat16).astype(jnp.float32)
    rest = x - high
    mid = rest.astype(jnp.bfloat16).astype(jnp.float32)
    return high, mid, rest - mid


def tiles_kernel(parts, listed, *refs):
    where_ref, near_ref, sigma_ref, eps_ref, charges_ref, types_ref = refs[:6]
    halves = refs[6 : 6 + 4 * parts]
    force_ref, energy_ref, cols, left, right, lbuf, rbuf = refs[6 + 4 * parts : 13 + 4 * parts]
    geos, turns, packs = [refs[13 + 4 * parts + 2 * i :][:2] for i in range(3)]
    width = halves[0].shape[2]
    atoms = cols.shape[1]
    row_tiles = width // TILE
    part = where_ref[0]
    first_tile = part * row_tiles

    kinds = types_ref[...]
    radius = jnp.zeros(kinds.shape, jnp.float32)
    depth = jnp.zeros(kinds.shape, jnp.float32)
    for level in range(sigma_ref.shape[0]):
        here = kinds == level
        radius = jnp.where(here, sigma_ref[level], radius)
        depth = jnp.where(here, eps_ref[level], depth)
    cols[3:4, :] = 0.5 * radius
    cols[10:16, :] = jnp.zeros((6, atoms), jnp.float32)
    base = 2.0 * jnp.sqrt(depth)
    spans = []
    for step in range(parts):
        start = pl.multiple_of(lax.rem(part + step, parts) * width, TILE)
        spans.append(pl.ds(start, width))
        cols[0:3, spans[step]] = halves[step][0] - 0.5
    for h in range(3):
        for step in range(parts):
            cols[4 + 2 * h : 6 + 2 * h, spans[step]] = halves[parts * (h + 1) + step][0]
        cols[4 + 2 * h : 5 + 2 * h, :] = cols[4 + 2 * h : 5 + 2 * h, :] * charges_ref[...]
        cols[5 + 2 * h : 6 + 2 * h, :] = cols[5 + 2 * h : 6 + 2 * h, :] * base

    chunk = lbuf.shape[1]
    lbuf[...] = jnp.zeros(lbuf.shape, jnp.float32)
    rbuf[...] = jnp.zeros(rbuf.shape, jnp.float32)
    lbuf[30:39, :] = jnp.ones((9, chunk), jnp.float32)
    rbuf[24:30, :] = jnp.ones((6, chunk), jnp.float32)
    soft_parts = split3(jnp.full((1, chunk), DELTA_SOFT, jnp.float32))
    for i in range(3):
        rbuf[36 + i : 37 + i, :] = soft_parts[i]
    row = lax.broadcasted_iota(jnp.int32, (DEPTH, TILE), 0)
    cross = row < 24
    radial = cross & (lax.rem(row, 4) == 3) | ((row >= 27) & (row < 30)) | ((row >= 33) & (row < 36))
    keep_u = (~radial) & (row < 39)
    keep_v = row < 36
    keeps = (keep_u, keep_v, radial)
    quad = lax.broadcasted_iota(jnp.int32, (4, chunk), 0)
    sign = jnp.where(quad == 3, 2.0, -2.0).astype(jnp.float32)

    def prepare(c, carry):
        span = pl.ds(pl.multiple_of(c * chunk, TILE), chunk)
        four = cols[0:4, span]
        square = four * four
        norm = split3(square[0:1] + square[1:2] + square[2:3])
        area = split3(square[3:4])
        high, mid, low = split3(four)
        shigh, smid, slow = high * sign, mid * sign, low * sign
        for i, v in enumerate((high, high, mid, mid, high, low)):
            lbuf[4 * i : 4 * i + 4, :] = v
        for i, v in enumerate((shigh, smid, shigh, smid, slow, shigh)):
            rbuf[4 * i : 4 * i + 4, :] = v
        for i in range(3):
            lbuf[24 + i : 25 + i, :] = norm[i]
            lbuf[27 + i : 28 + i, :] = area[i]
            rbuf[30 + i : 31 + i, :] = norm[i]
            rbuf[33 + i : 34 + i, :] = area[i]
        lbuf[40:41, :] = cols[4:5, span]
        lbuf[41:42, :] = 6.0 * cols[5:6, span]
        left[:, span] = lbuf[...]
        for i in range(chunk // TILE):
            block = rbuf[:, i * TILE : (i + 1) * TILE]
            for j in range(3):
                place = pl.multiple_of((c * (chunk // TILE) + i) * (3 * TILE) + j * TILE, TILE)
                right[:, pl.ds(place, TILE)] = jnp.where(keeps[j], block, 0.0).astype(jnp.bfloat16)
        return carry

    lax.fori_loop(0, atoms // chunk, prepare, 0)

    lane = lax.broadcasted_iota(jnp.int32, (SUB, TILE), 1)

    def geometry(t, s):
        own_span = pl.ds(pl.multiple_of((first_tile + t) * TILE, TILE), TILE)
        turned = left[:, own_span].T
        turns[s][...] = turned
        lhs = turned.astype(jnp.bfloat16)
        for k in range(listed):
            span = pl.ds(pl.multiple_of(near_ref[t, k] * (3 * TILE), TILE), 3 * TILE)
            geos[s][k] = jnp.dot(lhs, right[:, span], preferred_element_type=jnp.float32)

    def blocks(t, s, selfs):
        own = first_tile + t
        own_span = pl.ds(pl.multiple_of(own * TILE, TILE), TILE)
        near = [near_ref[t, k] for k in range(listed)]
        near_spans = [pl.ds(pl.multiple_of(n * TILE, TILE), TILE) for n in near]
        twice = jnp.float32(0.0)
        for n in near:
            twice = twice + (n == own).astype(jnp.float32)
        mine = cols[:, own_span]
        selfs = selfs + twice * (mine * mine)
        for b in range(TILE // SUB):
            rows = pl.ds(b * SUB, SUB)
            qi = jnp.broadcast_to(turns[s][rows, 40:41], (SUB, TILE))
            e6 = jnp.broadcast_to(turns[s][rows, 41:42], (SUB, TILE))
            sums = [None] * 10

            def put(slot, value):
                sums[slot] = value if sums[slot] is None else sums[slot] + value

            for k, span in enumerate(near_spans):
                def col(c):
                    return jnp.broadcast_to(cols[c : c + 1, span], (SUB, TILE))

                inv = lax.rsqrt(geos[s][k, rows, 0:TILE])
                root = lax.rsqrt(geos[s][k, rows, TILE : 2 * TILE])
                p = root * root
                x = geos[s][k, rows, 2 * TILE : 3 * TILE] * p
                x3 = x * x * x
                low = x3 - 1.0
                lj = x3 * low
                charge = col(4) * inv
                put(4, charge)
                put(5, col(5) * lj)
                put(6, col(6) * inv)
                put(7, col(7) * lj)
                put(8, col(8) * inv)
                put(9, col(9) * lj)
                w = qi * (charge * (inv * inv)) + (e6 * col(5)) * ((x3 * p) * (x3 + low))
                put(0, w * col(0))
                put(1, w * col(1))
                put(2, w * col(2))
                put(3, w)
            line = jnp.sum(sums[9], axis=1, keepdims=True)
            for c in range(8, -1, -1):
                line = jnp.where(lane == c, jnp.sum(sums[c], axis=1, keepdims=True), line)
            packs[s][rows, :] = line
        return selfs

    def finish(t, s, totals):
        own_span = pl.ds(pl.multiple_of((first_tile + t) * TILE, TILE), TILE)
        flat = packs[s][...].T[0:16]
        mine = cols[:, own_span]
        out_span = pl.ds(pl.multiple_of(t * TILE, TILE), TILE)
        force_ref[0, :, out_span] = mine[0:3] * flat[3:4] - flat[0:3]
        return totals + mine * flat

    def two_tiles(m, carry):
        totals, selfs = carry
        t = 2 * m
        totals = finish(jnp.maximum(t - 1, 0), 1, totals)
        geometry(t + 1, 1)
        selfs = blocks(t, 0, selfs)
        totals = finish(t, 0, totals)
        geometry(jnp.minimum(t + 2, row_tiles - 1), 0)
        selfs = blocks(t + 1, 1, selfs)
        return totals, selfs

    zero = jnp.zeros((16, TILE), jnp.float32)
    packs[1][...] = jnp.zeros(packs[1].shape, jnp.float32)
    geometry(0, 0)
    totals, selfs = lax.fori_loop(0, row_tiles // 2, two_tiles, (zero, zero))
    totals = finish(row_tiles - 1, 1, totals)
    soft = lax.rsqrt(jnp.full((1, TILE), DELTA_SOFT, jnp.float32))
    lane1 = lax.broadcasted_iota(jnp.int32, (1, TILE), 1)
    line = jnp.zeros((1, TILE), jnp.float32)
    for h in range(3):
        c = 4 + 2 * h
        value = jnp.sum(totals[c : c + 1] + totals[c + 1 : c + 2] - selfs[c : c + 1] * soft)
        line = jnp.where(lane1 == h, value, line)
    energy_ref[...] = line


def per_device(
    coords, velocities, coupling, charges, types, type_sigma, type_eps, near_tiles, accept
):
    parts, width = lax.axis_size("atom"), coords.shape[2]
    atoms = parts * width
    part = lax.axis_index("atom")
    halves = [coords] + [moved(coords, 0, step) for step in range(1, parts)]
    for by in (0, 1, -1):
        for step in range(parts):
            halves.append(coupling if by == step == 0 else moved(coupling, by, step))
    lower_coords, lower_moving = moved(coords, 1, 0), moved(velocities, 1, 0)
    upper_coords, upper_moving = moved(coords, -1, 0), moved(velocities, -1, 0)

    smem = pl.BlockSpec(memory_space=pltpu.SMEM)
    vmem = pl.BlockSpec(memory_space=pltpu.VMEM)
    pairs = width * near_tiles.shape[1] * TILE
    force, line = pl.pallas_call(
        partial(tiles_kernel, parts, near_tiles.shape[1]),
        out_shape=(
            jax.ShapeDtypeStruct(coords.shape, jnp.float32),
            jax.ShapeDtypeStruct((1, TILE), jnp.float32),
        ),
        in_specs=[smem] * 4 + [vmem] * (2 + len(halves)),
        out_specs=(vmem, vmem),
        scratch_shapes=[
            pltpu.VMEM((16, atoms), jnp.float32),
            pltpu.VMEM((DEPTH, atoms), jnp.float32),
            pltpu.VMEM((DEPTH, 3 * atoms), jnp.bfloat16),
            pltpu.VMEM((DEPTH, 4 * TILE), jnp.float32),
            pltpu.VMEM((DEPTH, 4 * TILE), jnp.float32),
        ]
        + [pltpu.VMEM((near_tiles.shape[1], TILE, 3 * TILE), jnp.float32)] * 2
        + [pltpu.VMEM((TILE, DEPTH), jnp.float32)] * 2
        + [pltpu.VMEM((TILE, TILE), jnp.float32)] * 2,
        cost_estimate=pl.CostEstimate(
            flops=50 * pairs, bytes_accessed=4 * 20 * atoms, transcendentals=2 * pairs
        ),
        name="tiles",
    )(
        part.reshape(1).astype(jnp.int32),
        near_tiles,
        type_sigma,
        type_eps,
        charges.reshape(1, atoms),
        types.reshape(1, atoms),
        *halves,
    )
    shares = jnp.stack([line[0, :3]] + [moved(line, 0, step)[0, :3] for step in range(1, parts)])
    total = shares[0]
    for step in range(1, parts):
        total = total + shares[step]
    if parts > 2:
        order = (jnp.arange(parts) - part) % parts
        total = jnp.sum(shares[order], axis=0)
    energies = (total * (0.5 / atoms))[None]

    replica, cycle = lax.axis_index("lam"), lax.axis_size("lam")
    up = accept[replica] == 1
    low = accept[(replica + cycle - 1) % cycle] == 1
    new_coords = jnp.where(up, upper_coords, jnp.where(low, lower_coords, coords))
    new_velocities = jnp.where(up, upper_moving, jnp.where(low, lower_moving, velocities))
    return (energies, force, new_coords, new_velocities)


def solution(mesh):
    split = P("lam", None, "atom")
    return jax.shard_map(
        per_device,
        mesh=mesh,
        in_specs=(split, split, split, P(), P(), P(), P(), P("atom", None), P()),
        out_specs=(P("lam", None), split, split, split),
        check_vma=False,
    )
```

time: 260 us -> 130 us (0.50)
  Pallas kernels: 233 us -> 103 us
    pallas_call x1, Pallas kernels: 233 us -> 103 us  [per_device(): pl.pallas_call(partial(tiles_kernel, parts, near_tiles.shape[1]), out_sha...]
  transfers between devices with their start and end apart: 11 -> 11, of which waited for: 1 -> 1; matrix products, arithmetic and copies ran while one was open for 2% -> 4% of each run, Pallas kernels for 90% -> 79%
where the time goes in v2:
time: 130 us
  Pallas kernels  103 us (79%)
  starting transfers between devices  16.2 us (12%)
  local copies, waits for them, and re-layouts  5.77 us (4%)
  other arithmetic  2.07 us (2%)
  between operations  1.97 us (2%)
    pallas_call x1, Pallas kernels, per_device(): pl.pallas_call(partial(tiles_kernel, parts, near_tiles.shape[1]), out_sha...  103 us
    ppermute x11, starting transfers between devices, moved(): return lax.ppermute(x, ('lam', 'atom'), pairs)  16.2 us
    unnamed x31, local copies, waits for them, and re-layouts  5.16 us
  transfers between devices with their start and end apart: 11, of which 1 were waited for; matrix products, arithmetic and copies ran while one was open for 4% of the time, Pallas kernels for 79%

profile of v2, /device:TPU:0, one launch (start us, length us, event | category | flops | bytes accessed | tf_op | source)
XLA Modules:
  0.0 130.1 jit_solution(15893868801178722428)
XLA Ops:
  0.6 0.0 copy-start.7
  0.6 0.0 copy-start
  0.7 0.0 copy-start.3
  0.7 3.1 %collective-permute-start.1 = (f32[1,2,8192]{2,1,0:T(2,128)}, f32[1,2,8192]{2,1,0:T(2,128)S(1)}, u32[]{:S(2)}, u32[]{:S(2)}) collective-permute-start(f32[1,2,8192]{2,1,0:T(2,128)} %refs_8_.1), channel_id=1, source_target_pairs={{1,0},{0,1},{3,2},{2,3},{5,4},{4,5},{7,6},{6,7},{9,8},{8,9},{11,10... | collective-permute-start | bytes 196616 | tf_op jit(solution)/shard_map/ppermute | solution.py:23
  3.7 0.0 collective-permute-start.2
  3.7 1.7 %collective-permute-start.3 = (f32[1,2,8192]{2,1,0:T(2,128)}, f32[1,2,8192]{2,1,0:T(2,128)S(1)}, u32[]{:S(2)}, u32[]{:S(2)}) collective-permute-start(f32[1,2,8192]{2,1,0:T(2,128)} %refs_8_.1), channel_id=1, source_target_pairs={{31,0},{30,1},{1,2},{0,3},{3,4},{2,5},{5,6},{4,7},{7,8},{6,9},{9,1... | collective-permute-start | bytes 196616 | tf_op jit(solution)/shard_map/ppermute | solution.py:23
  5.4 1.0 copy.15.refs_6_
  6.4 0.0 copy-start.1
  6.4 1.6 %collective-permute-start = (f32[1,3,8192]{2,1,0:T(4,128)S(1)}, f32[1,3,8192]{2,1,0:T(4,128)S(1)}, u32[]{:S(2)}, u32[]{:S(2)}) collective-permute-start(f32[1,3,8192]{2,1,0:T(4,128)S(1)} %copy.15.refs_6_), channel_id=1, source_target_pairs={{1,0},{0,1},{3,2},{2,3},{5,4},{4,5},{7,6},{6,7},{9,8},{8,9},{11,10... | collective-permute-start | bytes 294920 | tf_op jit(solution)/shard_map/ppermute | solution.py:23
  8.0 0.0 copy-done
  8.0 2.4 %collective-permute-start.7 = (f32[1,3,8192]{2,0,1:T(1,128)S(1)}, f32[1,3,8192]{2,0,1:T(1,128)S(1)}, u32[]{:S(2)}, u32[]{:S(2)}) collective-permute-start(f32[1,3,8192]{2,0,1:T(1,128)S(1)} %copy-done), channel_id=1, source_target_pairs={{2,0},{3,1},{4,2},{5,3},{6,4},{7,5},{8,6},{9,7},{10,8},{11,9},{12,... | collective-permute-start | bytes 294920 | tf_op jit(solution)/shard_map/ppermute | solution.py:23
  10.4 0.0 collective-permute-done.1.refs_9_
  10.4 0.0 copy-start.8
  10.4 0.0 collective-permute-start.8
  10.4 0.0 collective-permute-done.2.refs_10_
  10.4 0.0 copy-done.7
  10.4 0.0 copy-start.9
  10.4 4.5 %collective-permute-start.4 = (f32[1,2,8192]{2,1,0:T(2,128)S(1)}, f32[1,2,8192]{2,1,0:T(2,128)S(1)}, u32[]{:S(2)}, u32[]{:S(2)}) collective-permute-start(f32[1,2,8192]{2,1,0:T(2,128)S(1)} %copy-done.7), channel_id=1, source_target_pairs={{2,0},{3,1},{4,2},{5,3},{6,4},{7,5},{8,6},{9,7},{10,8},{11,9},{12,... | collective-permute-start | bytes 196616 | tf_op jit(solution)/shard_map/ppermute | solution.py:23
  14.9 0.0 collective-permute-done.3.refs_11_
  14.9 0.0 copy-start.10
  14.9 0.1 collective-permute-start.5
  15.0 0.0 copy-start.4
  15.0 0.7 copy-done.4
  15.7 0.7 copy.14.refs_1_
  16.4 0.0 copy-start.5
  16.4 0.7 copy-done.5
  17.0 0.6 fusion
  18.8 0.0 collective-permute-done.4.refs_12_
  18.8 0.0 copy-done.3
  18.8 0.0 copy-start.11
  18.9 2.4 %collective-permute-start.9 = (f32[1,3,8192]{2,0,1:T(1,128)S(1)}, f32[1,3,8192]{2,0,1:T(1,128)S(1)}, u32[]{:S(2)}, u32[]{:S(2)}) collective-permute-start(f32[1,3,8192]{2,0,1:T(1,128)S(1)} %copy-done.3), channel_id=1, source_target_pairs={{2,0},{3,1},{4,2},{5,3},{6,4},{7,5},{8,6},{9,7},{10,8},{11,9},{12,... | collective-permute-start | bytes 294920 | tf_op jit(solution)/shard_map/ppermute | solution.py:23
  21.3 0.0 collective-permute-done.5.refs_13_
  21.3 0.0 copy-start.12
  21.3 0.0 collective-permute-start.10
  21.3 0.0 collective-permute-done.refs_7_
  21.3 0.0 copy-start.6
  21.3 0.0 copy-done.1
  21.3 0.0 copy-done.8
  21.3 0.0 copy-done.9
  21.4 0.0 copy-done.10
  21.4 0.0 copy-done.11
  21.4 0.5 copy-done.12
  21.9 0.0 copy-done.6
  22.0 103.4 %tiles.1 = (f32[1,3,8192]{2,1,0:T(4,128)}, f32[1,128]{1,0:T(1,128)}) custom-call(s32[1]{0:T(128)} %bitcast.refs_0_, s32[64,5]{1,0:T(8,128)} %copy.14.refs_1_, f32[16]{0:T(128)} %refs_2_.1, f32[16]{0:T(128)} %refs_3_.1, f32[1,16384]{1,0:T(1,128)} %bitcast.5, s32[1,16384]{1,0:T(1,128)} %bitcast.6, f32[1,3,8192]{2,1,0:T(4,128)} %copy-done.1, ...), custom_call_target="tpu_custom_call" | custom-call | flops 262144000 | bytes 1310720 | tf_op jit(solution)/shard_map/tiles/pallas_call | solution.py:220
  125.3 0.0 copy-start.13
  125.3 0.7 copy-done.13
  126.0 0.5 collective-permute-start.6
  126.5 0.0 collective-permute-done.7
  126.5 0.0 collective-permute-done.8
  126.5 0.8 broadcast_select_fusion.3
  127.3 0.0 copy-start.2
  127.3 0.0 collective-permute-done.9
  127.3 0.0 collective-permute-done.10
  127.3 0.8 broadcast_select_fusion.2
  128.1 0.1 copy-done.2
  128.2 0.7 copy.16
  128.9 0.6 collective-permute-done.6
  129.6 0.5 add_multiply_fusion
Async XLA Ops:
  0.6 9.8 %copy-start.7 = (f32[1,2,8192]{2,1,0:T(2,128)S(1)}, f32[1,2,8192]{2,1,0:T(2,128)}, u32[]{:S(2)}) copy-start(f32[1,2,8192]{2,1,0:T(2,128)} %refs_8_.1) | copy-start | bytes 196612
  0.6 7.4 %copy-start = (f32[1,3,8192]{2,0,1:T(1,128)S(1)}, f32[1,3,8192]{2,0,1:T(1,128)}, u32[]{:S(2)}) copy-start(f32[1,3,8192]{2,0,1:T(1,128)} %param.9) | copy-start | bytes 294916
  0.7 18.2 %copy-start.3 = (f32[1,3,8192]{2,0,1:T(1,128)S(1)}, f32[1,3,8192]{2,0,1:T(1,128)}, u32[]{:S(2)}) copy-start(f32[1,3,8192]{2,0,1:T(1,128)} %param.10) | copy-start | bytes 294916
  0.7 9.7 %collective-permute-start.1 = (f32[1,2,8192]{2,1,0:T(2,128)}, f32[1,2,8192]{2,1,0:T(2,128)S(1)}, u32[]{:S(2)}, u32[]{:S(2)}) collective-permute-start(f32[1,2,8192]{2,1,0:T(2,128)} %refs_8_.1), channel_id=1, source_target_pairs={{1,0},{0,1},{3,2},{2,3},{5,4},{4,5},{7,6},{6,7},{9,8},{8,9},{11,10... | collective-permute-start | bytes 196616 | tf_op jit(solution)/shard_map/ppermute | solution.py:23
  3.7 6.7 %collective-permute-start.2 = (f32[1,2,8192]{2,1,0:T(2,128)}, f32[1,2,8192]{2,1,0:T(2,128)S(1)}, u32[]{:S(2)}, u32[]{:S(2)}) collective-permute-start(f32[1,2,8192]{2,1,0:T(2,128)} %refs_8_.1), channel_id=1, source_target_pairs={{30,0},{31,1},{0,2},{1,3},{2,4},{3,5},{4,6},{5,7},{6,8},{7,9},{8,1... | collective-permute-start | bytes 196616 | tf_op jit(solution)/shard_map/ppermute | solution.py:23
  3.7 11.2 %collective-permute-start.3 = (f32[1,2,8192]{2,1,0:T(2,128)}, f32[1,2,8192]{2,1,0:T(2,128)S(1)}, u32[]{:S(2)}, u32[]{:S(2)}) collective-permute-start(f32[1,2,8192]{2,1,0:T(2,128)} %refs_8_.1), channel_id=1, source_target_pairs={{31,0},{30,1},{1,2},{0,3},{3,4},{2,5},{5,6},{4,7},{7,8},{6,9},{9,1... | collective-permute-start | bytes 196616 | tf_op jit(solution)/shard_map/ppermute | solution.py:23
  6.4 14.9 %copy-start.1 = (f32[1,3,8192]{2,1,0:T(4,128)}, f32[1,3,8192]{2,1,0:T(4,128)S(1)}, u32[]{:S(2)}) copy-start(f32[1,3,8192]{2,1,0:T(4,128)S(1)} %copy.15.refs_6_) | copy-start | bytes 294916
  6.4 14.9 %collective-permute-start = (f32[1,3,8192]{2,1,0:T(4,128)S(1)}, f32[1,3,8192]{2,1,0:T(4,128)S(1)}, u32[]{:S(2)}, u32[]{:S(2)}) collective-permute-start(f32[1,3,8192]{2,1,0:T(4,128)S(1)} %copy.15.refs_6_), channel_id=1, source_target_pairs={{1,0},{0,1},{3,2},{2,3},{5,4},{4,5},{7,6},{6,7},{9,8},{8,9},{11,10... | collective-permute-start | bytes 294920 | tf_op jit(solution)/shard_map/ppermute | solution.py:23
  8.0 118.5 %collective-permute-start.7 = (f32[1,3,8192]{2,0,1:T(1,128)S(1)}, f32[1,3,8192]{2,0,1:T(1,128)S(1)}, u32[]{:S(2)}, u32[]{:S(2)}) collective-permute-start(f32[1,3,8192]{2,0,1:T(1,128)S(1)} %copy-done), channel_id=1, source_target_pairs={{2,0},{3,1},{4,2},{5,3},{6,4},{7,5},{8,6},{9,7},{10,8},{11,9},{12,... | collective-permute-start | bytes 294920 | tf_op jit(solution)/shard_map/ppermute | solution.py:23
  10.4 10.9 %copy-start.8 = (f32[1,2,8192]{2,1,0:T(2,128)}, f32[1,2,8192]{2,1,0:T(2,128)S(1)}, u32[]{:S(2)}) copy-start(f32[1,2,8192]{2,1,0:T(2,128)S(1)} %collective-permute-done.1.refs_9_) | copy-start | bytes 196612
  10.4 116.1 %collective-permute-start.8 = (f32[1,3,8192]{2,0,1:T(1,128)S(1)}, f32[1,3,8192]{2,0,1:T(1,128)S(1)}, u32[]{:S(2)}, u32[]{:S(2)}) collective-permute-start(f32[1,3,8192]{2,0,1:T(1,128)S(1)} %copy-done), channel_id=1, source_target_pairs={{30,0},{31,1},{0,2},{1,3},{2,4},{3,5},{4,6},{5,7},{6,8},{7,9},{8,1... | collective-permute-start | bytes 294920 | tf_op jit(solution)/shard_map/ppermute | solution.py:23
  10.4 10.9 %copy-start.9 = (f32[1,2,8192]{2,1,0:T(2,128)}, f32[1,2,8192]{2,1,0:T(2,128)S(1)}, u32[]{:S(2)}) copy-start(f32[1,2,8192]{2,1,0:T(2,128)S(1)} %collective-permute-done.2.refs_10_) | copy-start | bytes 196612
  10.4 8.4 %collective-permute-start.4 = (f32[1,2,8192]{2,1,0:T(2,128)S(1)}, f32[1,2,8192]{2,1,0:T(2,128)S(1)}, u32[]{:S(2)}, u32[]{:S(2)}) collective-permute-start(f32[1,2,8192]{2,1,0:T(2,128)S(1)} %copy-done.7), channel_id=1, source_target_pairs={{2,0},{3,1},{4,2},{5,3},{6,4},{7,5},{8,6},{9,7},{10,8},{11,9},{12,... | collective-permute-start | bytes 196616 | tf_op jit(solution)/shard_map/ppermute | solution.py:23
  14.9 6.5 %copy-start.10 = (f32[1,2,8192]{2,1,0:T(2,128)}, f32[1,2,8192]{2,1,0:T(2,128)S(1)}, u32[]{:S(2)}) copy-start(f32[1,2,8192]{2,1,0:T(2,128)S(1)} %collective-permute-done.3.refs_11_) | copy-start | bytes 196612
  14.9 6.4 %collective-permute-start.5 = (f32[1,2,8192]{2,1,0:T(2,128)S(1)}, f32[1,2,8192]{2,1,0:T(2,128)S(1)}, u32[]{:S(2)}, u32[]{:S(2)}) collective-permute-start(f32[1,2,8192]{2,1,0:T(2,128)S(1)} %copy-done.7), channel_id=1, source_target_pairs={{3,0},{2,1},{5,2},{4,3},{7,4},{6,5},{9,6},{8,7},{11,8},{10,9},{13,... | collective-permute-start | bytes 196616 | tf_op jit(solution)/shard_map/ppermute | solution.py:23
  15.0 0.7 copy-start.4
  16.4 0.7 copy-start.5
  18.8 2.5 %copy-start.11 = (f32[1,2,8192]{2,1,0:T(2,128)}, f32[1,2,8192]{2,1,0:T(2,128)S(1)}, u32[]{:S(2)}) copy-start(f32[1,2,8192]{2,1,0:T(2,128)S(1)} %collective-permute-done.4.refs_12_) | copy-start | bytes 196612
  18.9 108.4 %collective-permute-start.9 = (f32[1,3,8192]{2,0,1:T(1,128)S(1)}, f32[1,3,8192]{2,0,1:T(1,128)S(1)}, u32[]{:S(2)}, u32[]{:S(2)}) collective-permute-start(f32[1,3,8192]{2,0,1:T(1,128)S(1)} %copy-done.3), channel_id=1, source_target_pairs={{2,0},{3,1},{4,2},{5,3},{6,4},{7,5},{8,6},{9,7},{10,8},{11,9},{12,... | collective-permute-start | bytes 294920 | tf_op jit(solution)/shard_map/ppermute | solution.py:23
  21.3 0.6 copy-start.12
  21.3 106.0 %collective-permute-start.10 = (f32[1,3,8192]{2,0,1:T(1,128)S(1)}, f32[1,3,8192]{2,0,1:T(1,128)S(1)}, u32[]{:S(2)}, u32[]{:S(2)}) collective-permute-start(f32[1,3,8192]{2,0,1:T(1,128)S(1)} %copy-done.3), channel_id=1, source_target_pairs={{30,0},{31,1},{0,2},{1,3},{2,4},{3,5},{4,6},{5,7},{6,8},{7,9},{8,1... | collective-permute-start | bytes 294920 | tf_op jit(solution)/shard_map/ppermute | solution.py:23
  21.3 0.6 copy-start.6
  125.3 0.7 copy-start.13
  126.0 3.6 %collective-permute-start.6 = (f32[1,128]{1,0:T(1,128)S(1)}, f32[1,128]{1,0:T(1,128)S(1)}, u32[]{:S(2)}, u32[]{:S(2)}) collective-permute-start(f32[1,128]{1,0:T(1,128)S(1)} %copy-done.13), channel_id=1, source_target_pairs={{1,0},{0,1},{3,2},{2,3},{5,4},{4,5},{7,6},{6,7},{9,8},{8,9},{11,10... | collective-permute-start | bytes 1544 | tf_op jit(solution)/shard_map/ppermute | solution.py:23
  127.3 0.9 copy-start.2

commit v3 on v2

--- a/solution.py
+++ b/solution.py
@@ -30,11 +30,17 @@
     return high, mid, rest - mid
 
 
+def lane_sums(ones, x):
+    return lax.dot_general(
+        ones, x, (((1,), (1,)), ((), ())), preferred_element_type=jnp.float32
+    )
+
+
 def tiles_kernel(parts, listed, *refs):
     where_ref, near_ref, sigma_ref, eps_ref, charges_ref, types_ref = refs[:6]
     halves = refs[6 : 6 + 4 * parts]
     force_ref, energy_ref, cols, left, right, lbuf, rbuf = refs[6 + 4 * parts : 13 + 4 * parts]
-    geos, turns, packs = [refs[13 + 4 * parts + 2 * i :][:2] for i in range(3)]
+    geos, owns, accs = [refs[13 + 4 * parts + 2 * i :][:2] for i in range(3)]
     width = halves[0].shape[2]
     atoms = cols.shape[1]
     row_tiles = width // TILE
@@ -96,8 +102,11 @@
             lbuf[27 + i : 28 + i, :] = area[i]
             rbuf[30 + i : 31 + i, :] = norm[i]
             rbuf[33 + i : 34 + i, :] = area[i]
-        lbuf[40:41, :] = cols[4:5, span]
-        lbuf[41:42, :] = 6.0 * cols[5:6, span]
+        charge = split3(cols[4:5, span])
+        well = split3(6.0 * cols[5:6, span])
+        for i in range(3):
+            lbuf[40 + i : 41 + i, :] = charge[i]
+            lbuf[43 + i : 44 + i, :] = well[i]
         left[:, span] = lbuf[...]
         for i in range(chunk // TILE):
             block = rbuf[:, i * TILE : (i + 1) * TILE]
@@ -108,13 +117,17 @@
 
     lax.fori_loop(0, atoms // chunk, prepare, 0)
 
-    lane = lax.broadcasted_iota(jnp.int32, (SUB, TILE), 1)
+    side = lax.broadcasted_iota(jnp.int32, (DEPTH, 2 * TILE), 1) < TILE
+    deep = lax.broadcasted_iota(jnp.int32, (DEPTH, 2 * TILE), 0)
+    spread = jnp.where(
+        side & (deep >= 40) & (deep < 43) | (~side) & (deep >= 43) & (deep < 46), 1.0, 0.0
+    ).astype(jnp.bfloat16)
+    ones = jnp.ones((SUB, TILE), jnp.bfloat16)
 
     def geometry(t, s):
         own_span = pl.ds(pl.multiple_of((first_tile + t) * TILE, TILE), TILE)
-        turned = left[:, own_span].T
-        turns[s][...] = turned
-        lhs = turned.astype(jnp.bfloat16)
+        lhs = left[:, own_span].T.astype(jnp.bfloat16)
+        owns[s][...] = jnp.dot(lhs, spread, preferred_element_type=jnp.float32)
         for k in range(listed):
             span = pl.ds(pl.multiple_of(near_ref[t, k] * (3 * TILE), TILE), 3 * TILE)
             geos[s][k] = jnp.dot(lhs, right[:, span], preferred_element_type=jnp.float32)
@@ -131,8 +144,8 @@
         selfs = selfs + twice * (mine * mine)
         for b in range(TILE // SUB):
             rows = pl.ds(b * SUB, SUB)
-            qi = jnp.broadcast_to(turns[s][rows, 40:41], (SUB, TILE))
-            e6 = jnp.broadcast_to(turns[s][rows, 41:42], (SUB, TILE))
+            qi = owns[s][rows, 0:TILE]
+            e6 = owns[s][rows, TILE : 2 * TILE]
             sums = [None] * 10
 
             def put(slot, value):
@@ -161,19 +174,27 @@
                 put(1, w * col(1))
                 put(2, w * col(2))
                 put(3, w)
-            line = jnp.sum(sums[9], axis=1, keepdims=True)
-            for c in range(8, -1, -1):
-                line = jnp.where(lane == c, jnp.sum(sums[c], axis=1, keepdims=True), line)
-            packs[s][rows, :] = line
+            for c in range(10):
+                accs[s][c, rows, :] = sums[c]
         return selfs
 
     def finish(t, s, totals):
         own_span = pl.ds(pl.multiple_of((first_tile + t) * TILE, TILE), TILE)
-        flat = packs[s][...].T[0:16]
+        flat = []
+        for c in range(10):
+            whole = accs[s][c]
+            high = whole.astype(jnp.bfloat16)
+            rest = (whole - high.astype(jnp.float32)).astype(jnp.bfloat16)
+            flat.append(lane_sums(ones, high)[0:1] + lane_sums(ones, rest)[0:1])
         mine = cols[:, own_span]
         out_span = pl.ds(pl.multiple_of(t * TILE, TILE), TILE)
-        force_ref[0, :, out_span] = mine[0:3] * flat[3:4] - flat[0:3]
-        return totals + mine * flat
+        for c in range(3):
+            force_ref[0, c : c + 1, out_span] = mine[c : c + 1] * flat[3] - flat[c]
+        return tuple(
+            totals[h]
+            + (mine[4 + 2 * h : 5 + 2 * h] * flat[4 + 2 * h] + mine[5 + 2 * h : 6 + 2 * h] * flat[5 + 2 * h])
+            for h in range(3)
+        )
 
     def two_tiles(m, carry):
         totals, selfs = carry
@@ -187,16 +208,17 @@
         return totals, selfs
 
     zero = jnp.zeros((16, TILE), jnp.float32)
-    packs[1][...] = jnp.zeros(packs[1].shape, jnp.float32)
+    none = jnp.zeros((1, TILE), jnp.float32)
+    accs[1][...] = jnp.zeros(accs[1].shape, jnp.float32)
     geometry(0, 0)
-    totals, selfs = lax.fori_loop(0, row_tiles // 2, two_tiles, (zero, zero))
+    totals, selfs = lax.fori_loop(0, row_tiles // 2, two_tiles, ((none,) * 3, zero))
     totals = finish(row_tiles - 1, 1, totals)
     soft = lax.rsqrt(jnp.full((1, TILE), DELTA_SOFT, jnp.float32))
     lane1 = lax.broadcasted_iota(jnp.int32, (1, TILE), 1)
     line = jnp.zeros((1, TILE), jnp.float32)
     for h in range(3):
         c = 4 + 2 * h
-        value = jnp.sum(totals[c : c + 1] + totals[c + 1 : c + 2] - selfs[c : c + 1] * soft)
+        value = jnp.sum(totals[h] - selfs[c : c + 1] * soft)
         line = jnp.where(lane1 == h, value, line)
     energy_ref[...] = line
 
@@ -233,8 +255,8 @@
             pltpu.VMEM((DEPTH, 4 * TILE), jnp.float32),
         ]
         + [pltpu.VMEM((near_tiles.shape[1], TILE, 3 * TILE), jnp.float32)] * 2
-        + [pltpu.VMEM((TILE, DEPTH), jnp.float32)] * 2
-        + [pltpu.VMEM((TILE, TILE), jnp.float32)] * 2,
+        + [pltpu.VMEM((TILE, 2 * TILE), jnp.float32)] * 2
+        + [pltpu.VMEM((10, TILE, TILE), jnp.float32)] * 2,
         cost_estimate=pl.CostEstimate(
             flops=50 * pairs, bytes_accessed=4 * 20 * atoms, transcendentals=2 * pairs
         ),

time: 130 us -> 83.5 us (0.64)
  Pallas kernels: 103 us -> 56.6 us
    pallas_call x1, Pallas kernels: 103 us -> 56.6 us  [per_device(): pl.pallas_call(partial(tiles_kernel, parts, near_tiles.shape[1]), out_sha...]
  transfers between devices with their start and end apart: 11 -> 11, of which waited for: 1 -> 1; matrix products, arithmetic and copies ran while one was open for 4% -> 5% of each run, Pallas kernels for 79% -> 68%
where the time goes in v3:
time: 83.5 us; the launch traced here: 83.3 us
  Pallas kernels  56.6 us (68%)
  starting transfers between devices  16.3 us (20%)
  local copies, waits for them, and re-layouts  5.77 us (7%)
  other arithmetic  2.07 us (2%)
  between operations  1.97 us (2%)
    pallas_call x1, Pallas kernels, per_device(): pl.pallas_call(partial(tiles_kernel, parts, near_tiles.shape[1]), out_sha...  56.6 us
    ppermute x11, starting transfers between devices, moved(): return lax.ppermute(x, ('lam', 'atom'), pairs)  16.3 us
    unnamed x31, local copies, waits for them, and re-layouts  5.16 us
  transfers between devices with their start and end apart: 11, of which 1 were waited for; matrix products, arithmetic and copies ran while one was open for 5% of the time, Pallas kernels for 68%

profile of v3, /device:TPU:0, one launch (start us, length us, event | category | flops | bytes accessed | tf_op | source)
XLA Modules:
  0.0 83.3 jit_solution(1060608141310534400)
XLA Ops:
  0.6 0.0 copy-start.7
  0.6 0.0 copy-start
  0.7 0.0 copy-start.3
  0.7 3.1 %collective-permute-start.1 = (f32[1,2,8192]{2,1,0:T(2,128)}, f32[1,2,8192]{2,1,0:T(2,128)S(1)}, u32[]{:S(2)}, u32[]{:S(2)}) collective-permute-start(f32[1,2,8192]{2,1,0:T(2,128)} %refs_8_.1), channel_id=1, source_target_pairs={{1,0},{0,1},{3,2},{2,3},{5,4},{4,5},{7,6},{6,7},{9,8},{8,9},{11,10... | collective-permute-start | bytes 196616 | tf_op jit(solution)/shard_map/ppermute | solution.py:23
  3.7 0.0 collective-permute-start.2
  3.7 1.7 %collective-permute-start.3 = (f32[1,2,8192]{2,1,0:T(2,128)}, f32[1,2,8192]{2,1,0:T(2,128)S(1)}, u32[]{:S(2)}, u32[]{:S(2)}) collective-permute-start(f32[1,2,8192]{2,1,0:T(2,128)} %refs_8_.1), channel_id=1, source_target_pairs={{31,0},{30,1},{1,2},{0,3},{3,4},{2,5},{5,6},{4,7},{7,8},{6,9},{9,1... | collective-permute-start | bytes 196616 | tf_op jit(solution)/shard_map/ppermute | solution.py:23
  5.4 1.0 %copy.15.refs_6_ = f32[1,3,8192]{2,1,0:T(4,128)S(1)} copy(f32[1,3,8192]{2,0,1:T(1,128)} %param.9) | data formatting | bytes 196608 | tf_op args[0]
  6.4 0.0 copy-start.1
  6.4 1.6 %collective-permute-start = (f32[1,3,8192]{2,1,0:T(4,128)S(1)}, f32[1,3,8192]{2,1,0:T(4,128)S(1)}, u32[]{:S(2)}, u32[]{:S(2)}) collective-permute-start(f32[1,3,8192]{2,1,0:T(4,128)S(1)} %copy.15.refs_6_), channel_id=1, source_target_pairs={{1,0},{0,1},{3,2},{2,3},{5,4},{4,5},{7,6},{6,7},{9,8},{8,9},{11,10... | collective-permute-start | bytes 294920 | tf_op jit(solution)/shard_map/ppermute | solution.py:23
  8.0 0.0 copy-done
  8.0 2.4 %collective-permute-start.7 = (f32[1,3,8192]{2,0,1:T(1,128)S(1)}, f32[1,3,8192]{2,0,1:T(1,128)S(1)}, u32[]{:S(2)}, u32[]{:S(2)}) collective-permute-start(f32[1,3,8192]{2,0,1:T(1,128)S(1)} %copy-done), channel_id=1, source_target_pairs={{2,0},{3,1},{4,2},{5,3},{6,4},{7,5},{8,6},{9,7},{10,8},{11,9},{12,... | collective-permute-start | bytes 294920 | tf_op jit(solution)/shard_map/ppermute | solution.py:23
  10.4 0.0 collective-permute-done.1.refs_9_
  10.4 0.0 copy-start.8
  10.4 0.0 collective-permute-start.8
  10.4 0.0 collective-permute-done.2.refs_10_
  10.4 0.0 copy-done.7
  10.4 0.0 copy-start.9
  10.4 4.5 %collective-permute-start.4 = (f32[1,2,8192]{2,1,0:T(2,128)S(1)}, f32[1,2,8192]{2,1,0:T(2,128)S(1)}, u32[]{:S(2)}, u32[]{:S(2)}) collective-permute-start(f32[1,2,8192]{2,1,0:T(2,128)S(1)} %copy-done.7), channel_id=1, source_target_pairs={{2,0},{3,1},{4,2},{5,3},{6,4},{7,5},{8,6},{9,7},{10,8},{11,9},{12,... | collective-permute-start | bytes 196616 | tf_op jit(solution)/shard_map/ppermute | solution.py:23
  14.9 0.0 collective-permute-done.3.refs_11_
  14.9 0.0 copy-start.10
  14.9 0.1 collective-permute-start.5
  15.0 0.0 copy-start.4
  15.0 0.7 copy-done.4
  15.7 0.7 copy.14.refs_1_
  16.4 0.0 copy-start.5
  16.4 0.7 copy-done.5
  17.0 0.6 fusion
  18.8 0.0 collective-permute-done.4.refs_12_
  18.8 0.0 copy-done.3
  18.8 0.0 copy-start.11
  18.9 2.4 %collective-permute-start.9 = (f32[1,3,8192]{2,0,1:T(1,128)S(1)}, f32[1,3,8192]{2,0,1:T(1,128)S(1)}, u32[]{:S(2)}, u32[]{:S(2)}) collective-permute-start(f32[1,3,8192]{2,0,1:T(1,128)S(1)} %copy-done.3), channel_id=1, source_target_pairs={{2,0},{3,1},{4,2},{5,3},{6,4},{7,5},{8,6},{9,7},{10,8},{11,9},{12,... | collective-permute-start | bytes 294920 | tf_op jit(solution)/shard_map/ppermute | solution.py:23
  21.3 0.0 collective-permute-done.5.refs_13_
  21.3 0.0 copy-start.12
  21.3 0.0 collective-permute-start.10
  21.3 0.0 collective-permute-done.refs_7_
  21.3 0.0 copy-start.6
  21.3 0.0 copy-done.1
  21.3 0.0 copy-done.8
  21.3 0.0 copy-done.9
  21.4 0.0 copy-done.10
  21.4 0.0 copy-done.11
  21.4 0.5 copy-done.12
  21.9 0.0 copy-done.6
  22.0 56.6 %tiles.1 = (f32[1,3,8192]{2,1,0:T(4,128)}, f32[1,128]{1,0:T(1,128)}) custom-call(s32[1]{0:T(128)} %bitcast.refs_0_, s32[64,5]{1,0:T(8,128)} %copy.14.refs_1_, f32[16]{0:T(128)} %refs_2_.1, f32[16]{0:T(128)} %refs_3_.1, f32[1,16384]{1,0:T(1,128)} %bitcast.5, s32[1,16384]{1,0:T(1,128)} %bitcast.6, f32[1,3,8192]{2,1,0:T(4,128)} %copy-done.1, ...), custom_call_target="tpu_custom_call" | custom-call | flops 262144000 | bytes 1310720 | tf_op jit(solution)/shard_map/tiles/pallas_call | solution.py:242
  78.6 0.0 copy-start.13
  78.6 0.7 copy-done.13
  79.2 0.5 collective-permute-start.6
  79.8 0.0 collective-permute-done.7
  79.8 0.0 collective-permute-done.8
  79.8 0.8 broadcast_select_fusion.3
  80.6 0.0 copy-start.2
  80.6 0.0 collective-permute-done.9
  80.6 0.0 collective-permute-done.10
  80.6 0.8 broadcast_select_fusion.2
  81.4 0.1 copy-done.2
  81.5 0.7 copy.16
  82.2 0.6 collective-permute-done.6
  82.8 0.5 add_multiply_fusion
Async XLA Ops:
  0.6 9.8 %copy-start.7 = (f32[1,2,8192]{2,1,0:T(2,128)S(1)}, f32[1,2,8192]{2,1,0:T(2,128)}, u32[]{:S(2)}) copy-start(f32[1,2,8192]{2,1,0:T(2,128)} %refs_8_.1) | copy-start | bytes 196612
  0.6 7.4 %copy-start = (f32[1,3,8192]{2,0,1:T(1,128)S(1)}, f32[1,3,8192]{2,0,1:T(1,128)}, u32[]{:S(2)}) copy-start(f32[1,3,8192]{2,0,1:T(1,128)} %param.9) | copy-start | bytes 294916
  0.7 18.2 %copy-start.3 = (f32[1,3,8192]{2,0,1:T(1,128)S(1)}, f32[1,3,8192]{2,0,1:T(1,128)}, u32[]{:S(2)}) copy-start(f32[1,3,8192]{2,0,1:T(1,128)} %param.10) | copy-start | bytes 294916
  0.7 9.7 %collective-permute-start.1 = (f32[1,2,8192]{2,1,0:T(2,128)}, f32[1,2,8192]{2,1,0:T(2,128)S(1)}, u32[]{:S(2)}, u32[]{:S(2)}) collective-permute-start(f32[1,2,8192]{2,1,0:T(2,128)} %refs_8_.1), channel_id=1, source_target_pairs={{1,0},{0,1},{3,2},{2,3},{5,4},{4,5},{7,6},{6,7},{9,8},{8,9},{11,10... | collective-permute-start | bytes 196616 | tf_op jit(solution)/shard_map/ppermute | solution.py:23
  3.7 6.7 %collective-permute-start.2 = (f32[1,2,8192]{2,1,0:T(2,128)}, f32[1,2,8192]{2,1,0:T(2,128)S(1)}, u32[]{:S(2)}, u32[]{:S(2)}) collective-permute-start(f32[1,2,8192]{2,1,0:T(2,128)} %refs_8_.1), channel_id=1, source_target_pairs={{30,0},{31,1},{0,2},{1,3},{2,4},{3,5},{4,6},{5,7},{6,8},{7,9},{8,1... | collective-permute-start | bytes 196616 | tf_op jit(solution)/shard_map/ppermute | solution.py:23
  3.7 11.2 %collective-permute-start.3 = (f32[1,2,8192]{2,1,0:T(2,128)}, f32[1,2,8192]{2,1,0:T(2,128)S(1)}, u32[]{:S(2)}, u32[]{:S(2)}) collective-permute-start(f32[1,2,8192]{2,1,0:T(2,128)} %refs_8_.1), channel_id=1, source_target_pairs={{31,0},{30,1},{1,2},{0,3},{3,4},{2,5},{5,6},{4,7},{7,8},{6,9},{9,1... | collective-permute-start | bytes 196616 | tf_op jit(solution)/shard_map/ppermute | solution.py:23
  6.4 14.9 %copy-start.1 = (f32[1,3,8192]{2,1,0:T(4,128)}, f32[1,3,8192]{2,1,0:T(4,128)S(1)}, u32[]{:S(2)}) copy-start(f32[1,3,8192]{2,1,0:T(4,128)S(1)} %copy.15.refs_6_) | copy-start | bytes 294916
  6.4 14.9 %collective-permute-start = (f32[1,3,8192]{2,1,0:T(4,128)S(1)}, f32[1,3,8192]{2,1,0:T(4,128)S(1)}, u32[]{:S(2)}, u32[]{:S(2)}) collective-permute-start(f32[1,3,8192]{2,1,0:T(4,128)S(1)} %copy.15.refs_6_), channel_id=1, source_target_pairs={{1,0},{0,1},{3,2},{2,3},{5,4},{4,5},{7,6},{6,7},{9,8},{8,9},{11,10... | collective-permute-start | bytes 294920 | tf_op jit(solution)/shard_map/ppermute | solution.py:23
  8.0 71.8 %collective-permute-start.7 = (f32[1,3,8192]{2,0,1:T(1,128)S(1)}, f32[1,3,8192]{2,0,1:T(1,128)S(1)}, u32[]{:S(2)}, u32[]{:S(2)}) collective-permute-start(f32[1,3,8192]{2,0,1:T(1,128)S(1)} %copy-done), channel_id=1, source_target_pairs={{2,0},{3,1},{4,2},{5,3},{6,4},{7,5},{8,6},{9,7},{10,8},{11,9},{12,... | collective-permute-start | bytes 294920 | tf_op jit(solution)/shard_map/ppermute | solution.py:23
  10.4 10.9 %copy-start.8 = (f32[1,2,8192]{2,1,0:T(2,128)}, f32[1,2,8192]{2,1,0:T(2,128)S(1)}, u32[]{:S(2)}) copy-start(f32[1,2,8192]{2,1,0:T(2,128)S(1)} %collective-permute-done.1.refs_9_) | copy-start | bytes 196612
  10.4 69.4 %collective-permute-start.8 = (f32[1,3,8192]{2,0,1:T(1,128)S(1)}, f32[1,3,8192]{2,0,1:T(1,128)S(1)}, u32[]{:S(2)}, u32[]{:S(2)}) collective-permute-start(f32[1,3,8192]{2,0,1:T(1,128)S(1)} %copy-done), channel_id=1, source_target_pairs={{30,0},{31,1},{0,2},{1,3},{2,4},{3,5},{4,6},{5,7},{6,8},{7,9},{8,1... | collective-permute-start | bytes 294920 | tf_op jit(solution)/shard_map/ppermute | solution.py:23
  10.4 10.9 %copy-start.9 = (f32[1,2,8192]{2,1,0:T(2,128)}, f32[1,2,8192]{2,1,0:T(2,128)S(1)}, u32[]{:S(2)}) copy-start(f32[1,2,8192]{2,1,0:T(2,128)S(1)} %collective-permute-done.2.refs_10_) | copy-start | bytes 196612
  10.4 8.4 %collective-permute-start.4 = (f32[1,2,8192]{2,1,0:T(2,128)S(1)}, f32[1,2,8192]{2,1,0:T(2,128)S(1)}, u32[]{:S(2)}, u32[]{:S(2)}) collective-permute-start(f32[1,2,8192]{2,1,0:T(2,128)S(1)} %copy-done.7), channel_id=1, source_target_pairs={{2,0},{3,1},{4,2},{5,3},{6,4},{7,5},{8,6},{9,7},{10,8},{11,9},{12,... | collective-permute-start | bytes 196616 | tf_op jit(solution)/shard_map/ppermute | solution.py:23
  14.9 6.5 %copy-start.10 = (f32[1,2,8192]{2,1,0:T(2,128)}, f32[1,2,8192]{2,1,0:T(2,128)S(1)}, u32[]{:S(2)}) copy-start(f32[1,2,8192]{2,1,0:T(2,128)S(1)} %collective-permute-done.3.refs_11_) | copy-start | bytes 196612
  14.9 6.4 %collective-permute-start.5 = (f32[1,2,8192]{2,1,0:T(2,128)S(1)}, f32[1,2,8192]{2,1,0:T(2,128)S(1)}, u32[]{:S(2)}, u32[]{:S(2)}) collective-permute-start(f32[1,2,8192]{2,1,0:T(2,128)S(1)} %copy-done.7), channel_id=1, source_target_pairs={{3,0},{2,1},{5,2},{4,3},{7,4},{6,5},{9,6},{8,7},{11,8},{10,9},{13,... | collective-permute-start | bytes 196616 | tf_op jit(solution)/shard_map/ppermute | solution.py:23
  15.0 0.7 copy-start.4
  16.4 0.7 copy-start.5
  18.8 2.5 %copy-start.11 = (f32[1,2,8192]{2,1,0:T(2,128)}, f32[1,2,8192]{2,1,0:T(2,128)S(1)}, u32[]{:S(2)}) copy-start(f32[1,2,8192]{2,1,0:T(2,128)S(1)} %collective-permute-done.4.refs_12_) | copy-start | bytes 196612
  18.9 61.7 %collective-permute-start.9 = (f32[1,3,8192]{2,0,1:T(1,128)S(1)}, f32[1,3,8192]{2,0,1:T(1,128)S(1)}, u32[]{:S(2)}, u32[]{:S(2)}) collective-permute-start(f32[1,3,8192]{2,0,1:T(1,128)S(1)} %copy-done.3), channel_id=1, source_target_pairs={{2,0},{3,1},{4,2},{5,3},{6,4},{7,5},{8,6},{9,7},{10,8},{11,9},{12,... | collective-permute-start | bytes 294920 | tf_op jit(solution)/shard_map/ppermute | solution.py:23
  21.3 0.6 copy-start.12
  21.3 59.3 %collective-permute-start.10 = (f32[1,3,8192]{2,0,1:T(1,128)S(1)}, f32[1,3,8192]{2,0,1:T(1,128)S(1)}, u32[]{:S(2)}, u32[]{:S(2)}) collective-permute-start(f32[1,3,8192]{2,0,1:T(1,128)S(1)} %copy-done.3), channel_id=1, source_target_pairs={{30,0},{31,1},{0,2},{1,3},{2,4},{3,5},{4,6},{5,7},{6,8},{7,9},{8,1... | collective-permute-start | bytes 294920 | tf_op jit(solution)/shard_map/ppermute | solution.py:23
  21.3 0.6 copy-start.6
  78.6 0.7 copy-start.13
  79.2 3.6 %collective-permute-start.6 = (f32[1,128]{1,0:T(1,128)S(1)}, f32[1,128]{1,0:T(1,128)S(1)}, u32[]{:S(2)}, u32[]{:S(2)}) collective-permute-start(f32[1,128]{1,0:T(1,128)S(1)} %copy-done.13), channel_id=1, source_target_pairs={{1,0},{0,1},{3,2},{2,3},{5,4},{4,5},{7,6},{6,7},{9,8},{8,9},{11,10... | collective-permute-start | bytes 1544 | tf_op jit(solution)/shard_map/ppermute | solution.py:23
  80.6 0.9 %copy-start.2 = (f32[1,3,8192]{2,1,0:T(4,128)S(1)}, f32[1,3,8192]{2,1,0:T(4,128)}, u32[]{:S(2)}) copy-start(f32[1,3,8192]{2,1,0:T(4,128)} %get-tuple-element.9) | copy-start | bytes 294916

commit v4 on v3

--- a/solution.py
+++ b/solution.py
@@ -38,9 +38,9 @@
 
 def tiles_kernel(parts, listed, *refs):
     where_ref, near_ref, sigma_ref, eps_ref, charges_ref, types_ref = refs[:6]
-    halves = refs[6 : 6 + 4 * parts]
-    force_ref, energy_ref, cols, left, right, lbuf, rbuf = refs[6 + 4 * parts : 13 + 4 * parts]
-    geos, owns, accs = [refs[13 + 4 * parts + 2 * i :][:2] for i in range(3)]
+    halves = refs[6 : 6 + 3 * parts]
+    force_ref, energy_ref, cols, left, right, lbuf, rbuf = refs[6 + 3 * parts : 13 + 3 * parts]
+    geos, owns, accs = [refs[13 + 3 * parts + 2 * i :][:2] for i in range(3)]
     width = halves[0].shape[2]
     atoms = cols.shape[1]
     row_tiles = width // TILE
@@ -61,10 +61,12 @@
     for step in range(parts):
         start = pl.multiple_of(lax.rem(part + step, parts) * width, TILE)
         spans.append(pl.ds(start, width))
-        cols[0:3, spans[step]] = halves[step][0] - 0.5
+        cols[0:3, spans[step]] = halves[step][0, 0:3] - 0.5
     for h in range(3):
         for step in range(parts):
-            cols[4 + 2 * h : 6 + 2 * h, spans[step]] = halves[parts * (h + 1) + step][0]
+            block = halves[parts * h + step]
+            last = block.shape[1]
+            cols[4 + 2 * h : 6 + 2 * h, spans[step]] = block[0, last - 2 : last]
         cols[4 + 2 * h : 5 + 2 * h, :] = cols[4 + 2 * h : 5 + 2 * h, :] * charges_ref[...]
         cols[5 + 2 * h : 6 + 2 * h, :] = cols[5 + 2 * h : 6 + 2 * h, :] * base
 
@@ -122,7 +124,7 @@
     spread = jnp.where(
         side & (deep >= 40) & (deep < 43) | (~side) & (deep >= 43) & (deep < 46), 1.0, 0.0
     ).astype(jnp.bfloat16)
-    ones = jnp.ones((SUB, TILE), jnp.bfloat16)
+    ones = jnp.ones((SUB, 2 * TILE), jnp.bfloat16)
 
     def geometry(t, s):
         own_span = pl.ds(pl.multiple_of((first_tile + t) * TILE, TILE), TILE)
@@ -181,11 +183,14 @@
     def finish(t, s, totals):
         own_span = pl.ds(pl.multiple_of((first_tile + t) * TILE, TILE), TILE)
         flat = []
-        for c in range(10):
-            whole = accs[s][c]
-            high = whole.astype(jnp.bfloat16)
-            rest = (whole - high.astype(jnp.float32)).astype(jnp.bfloat16)
-            flat.append(lane_sums(ones, high)[0:1] + lane_sums(ones, rest)[0:1])
+        for c in range(0, 10, 2):
+            pair = []
+            for whole in (accs[s][c], accs[s][c + 1]):
+                high = whole.astype(jnp.bfloat16)
+                rest = (whole - high.astype(jnp.float32)).astype(jnp.bfloat16)
+                pair.append(jnp.concatenate([high, rest], axis=1))
+            both = lane_sums(ones, jnp.concatenate(pair, axis=0))
+            flat += [both[0:1, :TILE], both[0:1, TILE:]]
         mine = cols[:, own_span]
         out_span = pl.ds(pl.multiple_of(t * TILE, TILE), TILE)
         for c in range(3):
@@ -229,12 +234,14 @@
     parts, width = lax.axis_size("atom"), coords.shape[2]
     atoms = parts * width
     part = lax.axis_index("atom")
-    halves = [coords] + [moved(coords, 0, step) for step in range(1, parts)]
-    for by in (0, 1, -1):
-        for step in range(parts):
-            halves.append(coupling if by == step == 0 else moved(coupling, by, step))
-    lower_coords, lower_moving = moved(coords, 1, 0), moved(velocities, 1, 0)
-    upper_coords, upper_moving = moved(coords, -1, 0), moved(velocities, -1, 0)
+    packed = jnp.concatenate([coords, velocities, coupling], axis=1)
+    rows = jnp.concatenate([coords, coupling], axis=1)
+    lower, upper = moved(packed, 1, 0), moved(packed, -1, 0)
+    halves = [rows] + [moved(rows, 0, step) for step in range(1, parts)]
+    for by, block in ((1, lower), (-1, upper)):
+        halves.append(block)
+        for step in range(1, parts):
+            halves.append(moved(coupling, by, step))
 
     smem = pl.BlockSpec(memory_space=pltpu.SMEM)
     vmem = pl.BlockSpec(memory_space=pltpu.VMEM)
@@ -282,8 +289,8 @@
     replica, cycle = lax.axis_index("lam"), lax.axis_size("lam")
     up = accept[replica] == 1
     low = accept[(replica + cycle - 1) % cycle] == 1
-    new_coords = jnp.where(up, upper_coords, jnp.where(low, lower_coords, coords))
-    new_velocities = jnp.where(up, upper_moving, jnp.where(low, lower_moving, velocities))
+    new_coords = jnp.where(up, upper[:, 0:3], jnp.where(low, lower[:, 0:3], coords))
+    new_velocities = jnp.where(up, upper[:, 3:6], jnp.where(low, lower[:, 3:6], velocities))
     return (energies, force, new_coords, new_velocities)
 
 

time: 83.5 us -> 73.4 us (0.88)
  Pallas kernels: 56.6 us -> 48.4 us
  starting transfers between devices: 16.3 us -> 13 us
  local copies, waits for them, and re-layouts: 5.77 us -> 7.5 us
    pallas_call x1, Pallas kernels: 56.6 us -> 48.4 us  [per_device(): pl.pallas_call(partial(tiles_kernel, parts, near_tiles.shape[1]), out_sha...]
    ppermute x11 -> x6, starting transfers between devices: 16.3 us -> 13 us  [moved(): return lax.ppermute(x, ('lam', 'atom'), pairs)]
    unnamed x31 -> x32, local copies, waits for them, and re-layouts: 5.16 us -> 6.91 us
  transfers between devices with their start and end apart: 11 -> 6, of which waited for: 1 -> 0; matrix products, arithmetic and copies ran while one was open for 5% -> 7% of each run, Pallas kernels for 68% -> 0%
where the time goes in v4:
time: 73.4 us; the launch traced here: 73.1 us
  Pallas kernels  48.4 us (66%)
  starting transfers between devices  13 us (18%)
  local copies, waits for them, and re-layouts  7.5 us (10%)
  other arithmetic  2.12 us (3%)
  between operations  2.09 us (3%)
    pallas_call x1, Pallas kernels, per_device(): pl.pallas_call(partial(tiles_kernel, parts, near_tiles.shape[1]), out_sha...  48.4 us
    ppermute x6, starting transfers between devices, moved(): return lax.ppermute(x, ('lam', 'atom'), pairs)  13 us
    unnamed x32, local copies, waits for them, and re-layouts  6.91 us
  transfers between devices with their start and end apart: 6, of which 0 were waited for; matrix products, arithmetic and copies ran while one was open for 7% of the time, Pallas kernels for 0%

profile of v4, /device:TPU:0, one launch (start us, length us, event | category | flops | bytes accessed | tf_op | source)
XLA Modules:
  0.0 73.1 jit_solution(3106498065340281436)
XLA Ops:
  0.6 0.0 copy-start.1
  0.6 1.0 %copy.13 = f32[1,3,8192]{2,1,0:T(4,128)S(1)} copy(f32[1,3,8192]{2,0,1:T(1,128)} %param.9) | data formatting | bytes 196608 | tf_op args[0]
  1.6 0.0 copy-done.1
  1.7 0.0 copy-start.4
  1.7 0.1 copy.15
  1.7 0.8 %copy-done.4 = f32[1,2,8192]{2,1,0:T(2,128)S(1)} copy-done((f32[1,2,8192]{2,1,0:T(2,128)S(1)}, f32[1,2,8192]{2,1,0:T(2,128)}, u32[]{:S(2)}) %copy-start.4) | copy-done | bytes 65560
  2.5 0.1 pad_maximum_fusion.1
  2.6 0.5 collective-permute-start.1
  3.1 5.0 %collective-permute-start.3 = (f32[1,8,8192]{2,1,0:T(8,128)S(1)}, f32[1,8,8192]{2,1,0:T(8,128)S(1)}, u32[]{:S(2)}, u32[]{:S(2)}) collective-permute-start(f32[1,8,8192]{2,1,0:T(8,128)S(1)} %pad_maximum_fusion.1), channel_id=1, source_target_pairs={{2,0},{3,1},{4,2},{5,3},{6,4},{7,5},{8,6},{9,7},{10,8},{11,9},{12,... | collective-permute-start | bytes 786440 | tf_op jit(solution)/shard_map/ppermute | solution.py:23
  8.2 0.1 pad_maximum_fusion.refs_6_
  8.2 0.0 copy-start.5
  8.2 2.0 %collective-permute-start = (f32[1,5,8192]{2,1,0:T(8,128)S(1)}, f32[1,5,8192]{2,1,0:T(8,128)S(1)}, u32[]{:S(2)}, u32[]{:S(2)}) collective-permute-start(f32[1,5,8192]{2,1,0:T(8,128)S(1)} %pad_maximum_fusion.refs_6_), channel_id=1, source_target_pairs={{1,0},{0,1},{3,2},{2,3},{5,4},{4,5},{7,6},{6,7},{9,8},{8,9},{11,10... | collective-permute-start | bytes 491528 | tf_op jit(solution)/shard_map/ppermute | solution.py:23
  10.2 0.0 collective-permute-start.2
  10.2 5.3 %collective-permute-start.4 = (f32[1,2,8192]{2,1,0:T(2,128)S(1)}, f32[1,2,8192]{2,1,0:T(2,128)S(1)}, u32[]{:S(2)}, u32[]{:S(2)}) collective-permute-start(f32[1,2,8192]{2,1,0:T(2,128)S(1)} %copy-done.4), channel_id=1, source_target_pairs={{3,0},{2,1},{5,2},{4,3},{7,4},{6,5},{9,6},{8,7},{11,8},{10,9},{13,... | collective-permute-start | bytes 196616 | tf_op jit(solution)/shard_map/ppermute | solution.py:23
  15.6 0.0 copy-start.7
  15.6 0.7 copy-done.7
  16.2 0.0 copy-start.8
  16.2 0.7 copy.16.refs_1_
  17.0 0.0 copy-done.8
  17.0 0.6 fusion.2
  18.8 0.0 collective-permute-done.2.refs_9_
  18.9 0.0 copy-start.10
  18.9 0.0 collective-permute-done.4.refs_11_
  18.9 0.0 copy-start.11
  18.9 0.0 collective-permute-done.refs_7_
  18.9 0.0 copy-start.9
  18.9 0.0 collective-permute-done.1.refs_8_
  18.9 0.0 copy-start.2
  18.9 0.0 collective-permute-done.3.refs_10_
  18.9 0.0 copy-start.3
  19.0 0.0 copy-done.5
  19.0 0.5 copy-done.10
  19.5 0.0 copy-done.11
  19.5 0.1 copy-done.9
  19.6 0.1 copy-done.2
  19.7 0.1 copy-done.3
  19.8 0.0 copy-start
  19.8 48.4 %tiles.1 = (f32[1,3,8192]{2,1,0:T(4,128)}, f32[1,128]{1,0:T(1,128)}) custom-call(s32[1]{0:T(128)} %bitcast.refs_0_, s32[64,5]{1,0:T(8,128)} %copy.16.refs_1_, f32[16]{0:T(128)} %refs_2_.1, f32[16]{0:T(128)} %refs_3_.1, f32[1,16384]{1,0:T(1,128)} %bitcast.5, s32[1,16384]{1,0:T(1,128)} %bitcast.6, f32[1,5,8192]{2,1,0:T(8,128)} %copy-done.5, ...), custom_call_target="tpu_custom_call" | custom-call | flops 262144000 | bytes 1310720 | tf_op jit(solution)/shard_map/tiles/pallas_call | solution.py:249
  68.1 0.0 copy-start.12
  68.1 0.6 copy-done.12
  68.8 0.1 collective-permute-start.5
  68.8 0.0 copy-done
  68.9 0.0 copy-start.6
  68.9 1.5 %fusion = (f32[1,3,8192]{2,1,0:T(4,128)S(1)}, f32[1,3,8192]{2,1,0:T(4,128)S(1)}) fusion(f32[1,8,8192]{2,1,0:T(8,128)} %copy-done.2, f32[1,8,8192]{2,1,0:T(8,128)} %copy-done.3, pred[]{:T(512)} %bitcast.4, pred[]{:T(512)} %bitcast.3, f32[1,3,8192]{2,0,1:T(1,128)S(1)} %copy-done.1, f32[1,3,8192]{2,0,1:T(1,128)S(1)} %copy-done), kind=kLoop, calls=%fused_computation.3 | loop fusion | flops 98304 | bytes 786434 | tf_op jit(solution)/shard_map/jit(_where)/select_n | solution.py:293
  70.3 0.0 copy-done.6
  70.3 0.7 %copy.19 = f32[1,3,8192]{2,0,1:T(1,128)} copy(f32[1,3,8192]{2,1,0:T(4,128)S(1)} %copy-done.6) | data formatting | bytes 196608
  71.1 0.7 %copy.20 = f32[1,3,8192]{2,0,1:T(1,128)} copy(f32[1,3,8192]{2,1,0:T(4,128)S(1)} %get-tuple-element.13) | data formatting | bytes 196608
  71.8 0.7 %copy.21 = f32[1,3,8192]{2,0,1:T(1,128)} copy(f32[1,3,8192]{2,1,0:T(4,128)S(1)} %get-tuple-element.12) | data formatting | bytes 196608
  72.6 0.0 collective-permute-done.5
  72.6 0.5 add_multiply_fusion
Async XLA Ops:
  0.6 1.0 %copy-start.1 = (f32[1,3,8192]{2,0,1:T(1,128)S(1)}, f32[1,3,8192]{2,0,1:T(1,128)}, u32[]{:S(2)}) copy-start(f32[1,3,8192]{2,0,1:T(1,128)} %param.10) | copy-start | bytes 294916
  1.7 0.8 %copy-start.4 = (f32[1,2,8192]{2,1,0:T(2,128)S(1)}, f32[1,2,8192]{2,1,0:T(2,128)}, u32[]{:S(2)}) copy-start(f32[1,2,8192]{2,1,0:T(2,128)} %param.11) | copy-start | bytes 196612
  2.6 16.3 %collective-permute-start.1 = (f32[1,8,8192]{2,1,0:T(8,128)S(1)}, f32[1,8,8192]{2,1,0:T(8,128)S(1)}, u32[]{:S(2)}, u32[]{:S(2)}) collective-permute-start(f32[1,8,8192]{2,1,0:T(8,128)S(1)} %pad_maximum_fusion.1), channel_id=1, source_target_pairs={{30,0},{31,1},{0,2},{1,3},{2,4},{3,5},{4,6},{5,7},{6,8},{7,9},{8,1... | collective-permute-start | bytes 786440 | tf_op jit(solution)/shard_map/ppermute | solution.py:23
  3.1 15.8 %collective-permute-start.3 = (f32[1,8,8192]{2,1,0:T(8,128)S(1)}, f32[1,8,8192]{2,1,0:T(8,128)S(1)}, u32[]{:S(2)}, u32[]{:S(2)}) collective-permute-start(f32[1,8,8192]{2,1,0:T(8,128)S(1)} %pad_maximum_fusion.1), channel_id=1, source_target_pairs={{2,0},{3,1},{4,2},{5,3},{6,4},{7,5},{8,6},{9,7},{10,8},{11,9},{12,... | collective-permute-start | bytes 786440 | tf_op jit(solution)/shard_map/ppermute | solution.py:23
  8.2 10.7 %copy-start.5 = (f32[1,5,8192]{2,1,0:T(8,128)}, f32[1,5,8192]{2,1,0:T(8,128)S(1)}, u32[]{:S(2)}) copy-start(f32[1,5,8192]{2,1,0:T(8,128)S(1)} %pad_maximum_fusion.refs_6_) | copy-start | bytes 491524
  8.2 10.7 %collective-permute-start = (f32[1,5,8192]{2,1,0:T(8,128)S(1)}, f32[1,5,8192]{2,1,0:T(8,128)S(1)}, u32[]{:S(2)}, u32[]{:S(2)}) collective-permute-start(f32[1,5,8192]{2,1,0:T(8,128)S(1)} %pad_maximum_fusion.refs_6_), channel_id=1, source_target_pairs={{1,0},{0,1},{3,2},{2,3},{5,4},{4,5},{7,6},{6,7},{9,8},{8,9},{11,10... | collective-permute-start | bytes 491528 | tf_op jit(solution)/shard_map/ppermute | solution.py:23
  10.2 8.6 %collective-permute-start.2 = (f32[1,2,8192]{2,1,0:T(2,128)S(1)}, f32[1,2,8192]{2,1,0:T(2,128)S(1)}, u32[]{:S(2)}, u32[]{:S(2)}) collective-permute-start(f32[1,2,8192]{2,1,0:T(2,128)S(1)} %copy-done.4), channel_id=1, source_target_pairs={{31,0},{30,1},{1,2},{0,3},{3,4},{2,5},{5,6},{4,7},{7,8},{6,9},{9,1... | collective-permute-start | bytes 196616 | tf_op jit(solution)/shard_map/ppermute | solution.py:23
  10.2 8.7 %collective-permute-start.4 = (f32[1,2,8192]{2,1,0:T(2,128)S(1)}, f32[1,2,8192]{2,1,0:T(2,128)S(1)}, u32[]{:S(2)}, u32[]{:S(2)}) collective-permute-start(f32[1,2,8192]{2,1,0:T(2,128)S(1)} %copy-done.4), channel_id=1, source_target_pairs={{3,0},{2,1},{5,2},{4,3},{7,4},{6,5},{9,6},{8,7},{11,8},{10,9},{13,... | collective-permute-start | bytes 196616 | tf_op jit(solution)/shard_map/ppermute | solution.py:23
  15.6 0.7 copy-start.7
  16.2 0.7 copy-start.8
  18.9 0.6 copy-start.10
  18.9 0.6 copy-start.11
  18.9 0.7 copy-start.9
  18.9 0.8 %copy-start.2 = (f32[1,8,8192]{2,1,0:T(8,128)}, f32[1,8,8192]{2,1,0:T(8,128)S(1)}, u32[]{:S(2)}) copy-start(f32[1,8,8192]{2,1,0:T(8,128)S(1)} %collective-permute-done.1.refs_8_) | copy-start | bytes 786436
  18.9 0.8 %copy-start.3 = (f32[1,8,8192]{2,1,0:T(8,128)}, f32[1,8,8192]{2,1,0:T(8,128)S(1)}, u32[]{:S(2)}) copy-start(f32[1,8,8192]{2,1,0:T(8,128)S(1)} %collective-permute-done.3.refs_10_) | copy-start | bytes 786436
  19.8 49.1 %copy-start = (f32[1,3,8192]{2,0,1:T(1,128)S(1)}, f32[1,3,8192]{2,0,1:T(1,128)}, u32[]{:S(2)}) copy-start(f32[1,3,8192]{2,0,1:T(1,128)} %param.9) | copy-start | bytes 294916
  68.1 0.6 copy-start.12
  68.8 3.8 %collective-permute-start.5 = (f32[1,128]{1,0:T(1,128)S(1)}, f32[1,128]{1,0:T(1,128)S(1)}, u32[]{:S(2)}, u32[]{:S(2)}) collective-permute-start(f32[1,128]{1,0:T(1,128)S(1)} %copy-done.12), channel_id=1, source_target_pairs={{1,0},{0,1},{3,2},{2,3},{5,4},{4,5},{7,6},{6,7},{9,8},{8,9},{11,10... | collective-permute-start | bytes 1544 | tf_op jit(solution)/shard_map/ppermute | solution.py:23
  68.9 1.5 %copy-start.6 = (f32[1,3,8192]{2,1,0:T(4,128)S(1)}, f32[1,3,8192]{2,1,0:T(4,128)}, u32[]{:S(2)}) copy-start(f32[1,3,8192]{2,1,0:T(4,128)} %get-tuple-element.9) | copy-start | bytes 294916
